TPU v7x, 32 devices: a whole 2x2x4 slice. The times are simulated.
32 devices in a mesh: ha: 2 (over y), wa: 16 (over z, x, core).
Axes of the slice: x: 2, y: 2, z: 4, core: 2. Of those that a mesh axis runs over, the one named last changes fastest.
Arguments:
- query_field: float32 [2, 32, 64, 256], P(None, 'ha', 'wa'), may hold values from -150 to 150, as said below
- key_field: float32 [2, 32, 64, 256], P(None, 'ha', 'wa'), may hold values from -6 to 6
- value_field: float32 [2, 32, 64, 256], P(None, 'ha', 'wa'), may hold values from -6 to 6
- output_grad: float32 [2, 32, 64, 256], P(None, 'ha', 'wa'), may hold values from -6 to 6
Outputs:
- query_grad: float32 [2, 32, 64, 256], P(None, 'ha', 'wa')
- key_grad: float32 [2, 32, 64, 256], P(None, 'ha', 'wa')
- value_grad: float32 [2, 32, 64, 256], P(None, 'ha', 'wa')
Inputs may be any that keep to these rules, and one draw needn't show every extreme that they name: `query_field`: queries and keys are real-valued with no structure promised.
All inputs are finite; a program needn't handle non-finite values.
Results may differ from a plain program's by a relative error of at most 0.0003.
Values sent between devices are 32-bit elements; how exact they have to be, the bound alone decides.
No kernel may reach another device: no remote copies, remote signals or barrier semaphores. Data moves between devices by JAX's collectives and lax.ppermute only.
A program may use at most 128 MiB of HBM per device.

v0:
```python
import jax
import jax.numpy as jnp
from jax import lax
from jax.sharding import PartitionSpec as P

HEADS = 2
HEAD_DIM = 128
TILE = 16


def passed_along(block, axis, distance):
    devices = range(lax.axis_size(axis))
    route = [(i - distance, i) for i in devices if i - distance in devices]
    return lax.ppermute(block, axis, route)


def extended_2(value, sides, width):
    for axis, dim in sides:
        devices, length = (lax.axis_size(axis), value.shape[dim])
        up = [(i, (i + 1) % devices) for i in range(devices - 1)]
        down = [(j, i) for i, j in up]
        last = lax.slice_in_dim(value, length - width, length, axis=dim)
        first = lax.slice_in_dim(value, 0, width, axis=dim)
        before = lax.ppermute(last, axis, up)
        after = lax.ppermute(first, axis, down)
        value = jnp.concatenate([before, value, after], axis=dim)
    return value


def tile_grads(query_rows, grad_rows, key_rows, value_rows, key_valid):
    score_scale = HEAD_DIM ** (-0.5)
    highest = lax.Precision.HIGHEST
    mask_bias = jnp.where(key_valid, jnp.float32(0.0), jnp.float32(-1e30))
    query_parts = []
    key_parts = []
    value_parts = []
    for head_index in range(HEADS):
        head_start = head_index * HEAD_DIM
        head_stop = head_start + HEAD_DIM
        query_scaled = query_rows[:, head_start:head_stop] * score_scale
        grad_head = grad_rows[:, head_start:head_stop]
        key_head = key_rows[:, head_start:head_stop]
        value_head = value_rows[:, head_start:head_stop]
        scores = jnp.dot(query_scaled, key_head.T, precision=highest) + mask_bias[None, :]
        row_peak = jnp.max(scores, axis=1, keepdims=True)
        weights = jnp.exp(scores - row_peak)
        inverse = 1.0 / jnp.sum(weights, axis=1, keepdims=True)
        probabilities = weights * inverse
        dprobs = jnp.dot(grad_head, value_head.T, precision=highest)
        center = jnp.sum(probabilities * dprobs, axis=1, keepdims=True)
        dscores = probabilities * (dprobs - center)
        query_parts.append(jnp.dot(dscores, key_head, precision=highest) * score_scale)
        key_parts.append(jnp.dot(dscores.T, query_scaled, precision=highest))
        value_parts.append(jnp.dot(probabilities.T, grad_head, precision=highest))
    return (
        jnp.concatenate(query_parts, axis=1),
        jnp.concatenate(key_parts, axis=1),
        jnp.concatenate(value_parts, axis=1),
    )


def widen(source, pieces, reach):
    return jnp.concatenate(pieces[:reach] + [source] + pieces[reach:], axis=3)


def width_slices(source, reach, cols_local):
    margin = reach * cols_local
    slices = []
    for slot in range(2 * reach):
        if slot < reach:
            begin = slot * cols_local
        else:
            begin = margin + cols_local + (slot - reach) * cols_local
        slices.append(source[:, :, :, begin : begin + cols_local])
    return slices


def settle_rows(source, from_below, from_above, rows_local):
    inner = source[:, :, TILE : TILE + rows_local]
    return inner + from_below + from_above


def body(query_field, key_field, value_field, output_grad):
    frames, rows_local, cols_local, channels = query_field.shape
    reach = (max(2 * TILE - cols_local, TILE) + cols_local - 1) // cols_local
    margin = reach * cols_local
    height_index = lax.axis_index("ha")
    width_index = lax.axis_index("wa")
    height_total = rows_local * lax.axis_size("ha")
    width_total = cols_local * lax.axis_size("wa")
    offsets = list(range(reach, 0, -1)) + list(range(-1, -reach - 1, -1))
    stacked = jnp.stack([key_field, value_field])
    anchor = jnp.int32(0)
    first_col = width_index * cols_local
    tile_col = first_col // TILE
    column_start = margin - first_col % TILE - TILE
    pieces = []
    for distance in offsets:
        pieces.append(passed_along(stacked, "wa", distance))
    trimmed = lax.dynamic_slice_in_dim(widen(stacked, pieces, reach), column_start, 3 * TILE, 3)
    extended = extended_2(trimmed, (("ha", 2),), TILE)
    window_span = jnp.arange(3 * TILE, dtype=jnp.int32)
    cols_global = tile_col * TILE - TILE + window_span
    col_ok = (cols_global >= 0) & (cols_global < width_total)
    window_shape = (2, frames, 3 * TILE, 3 * TILE, channels)
    query_rows = query_field.reshape(-1, channels)
    grad_rows = output_grad.reshape(-1, channels)
    key_rows = extended[0].reshape(-1, channels)
    value_rows = extended[1].reshape(-1, channels)
    rows_global = height_index * rows_local + 0 - TILE + window_span
    row_ok = (rows_global >= 0) & (rows_global < height_total)
    plane_ok = row_ok[:, None] & col_ok[None, :]
    key_valid = jnp.broadcast_to(plane_ok[None], (frames, 3 * TILE, 3 * TILE)).reshape(-1)
    query_part, key_part, value_part = tile_grads(
        query_rows, grad_rows, key_rows, value_rows, key_valid
    )
    update = jnp.stack([key_part, value_part]).reshape(window_shape)
    query_blocks = query_part.reshape(frames, TILE, cols_local, channels)
    rims = []
    for rim_part, distance in ((update[:, :, :TILE], -1), (update[:, :, TILE + rows_local :], 1)):
        rims.append(passed_along(rim_part, "ha", distance))
    settled_window = settle_rows(update, rims[0], rims[1], rows_local)
    frame_shape = (2, frames, rows_local, cols_local + 2 * margin, channels)
    settled = lax.dynamic_update_slice(
        jnp.zeros(frame_shape, jnp.float32),
        settled_window,
        (anchor, anchor, anchor, column_start, anchor),
    )
    final = settled[:, :, :, margin : margin + cols_local]
    slices = width_slices(settled, reach, cols_local)
    for slot in range(2 * reach):
        final = final + passed_along(slices[slot], "wa", -offsets[slot])
    return (query_blocks, final[0], final[1])


def solution(mesh):
    placed = (
        P(None, "ha", "wa", None),
        P(None, "ha", "wa", None),
        P(None, "ha", "wa", None),
        P(None, "ha", "wa", None),
    )
    return jax.shard_map(
        body,
        mesh=mesh,
        in_specs=placed,
        out_specs=(P(None, "ha", "wa", None), P(None, "ha", "wa", None), P(None, "ha", "wa", None)),
        check_vma=False,
    )
```

profile of v0, /device:TPU:1, one launch (start us, length us, event | category | flops | bytes accessed | tf_op | source)
XLA Modules:
  0.0 430.5 jit_solution(7500678265862068468)
XLA Ops:
  1.7 5.6 %collective-permute-start = (f32[2,2,16,4,256]{4,3,2,1,0:T(4,128)S(1)}, f32[2,2,16,4,256]{4,3,2,1,0:T(4,128)S(1)}, u32[]{:S(2)}, u32[]{:S(2)}) collective-permute-start(f32[2,2,16,4,256]{4,3,2,1,0:T(4,128)S(1)} %pad_maximum_fusion.4), channel_id=1, source_target_pairs={{0,7},{1,8},{2,9},{3,10},{4,11},{5,12},{6,13},{7,14},{8,15},{16,23... | collective-permute-start | bytes 786440 | tf_op jit(solution)/shard_map/ppermute | solution.py:14
  38.2 4.8 %collective-permute-done.8 = f32[2,2,16,4,256]{4,3,2,1,0:T(4,128)S(1)} collective-permute-done((f32[2,2,16,4,256]{4,3,2,1,0:T(4,128)S(1)}, f32[2,2,16,4,256]{4,3,2,1,0:T(4,128)S(1)}, u32[]{:S(2)}, u32[]{:S(2)}) %collective-permute-start.8) | collective-permute-done | bytes 262176 | tf_op jit(solution)/shard_map/ppermute | solution.py:14
  44.3 10.1 %collective-permute-done.9 = f32[2,2,16,4,256]{4,3,2,1,0:T(4,128)S(1)} collective-permute-done((f32[2,2,16,4,256]{4,3,2,1,0:T(4,128)S(1)}, f32[2,2,16,4,256]{4,3,2,1,0:T(4,128)S(1)}, u32[]{:S(2)}, u32[]{:S(2)}) %collective-permute-start.9) | collective-permute-done | bytes 262176 | tf_op jit(solution)/shard_map/ppermute | solution.py:14
  54.4 5.1 %collective-permute-done.10 = f32[2,2,16,4,256]{4,3,2,1,0:T(4,128)S(1)} collective-permute-done((f32[2,2,16,4,256]{4,3,2,1,0:T(4,128)S(1)}, f32[2,2,16,4,256]{4,3,2,1,0:T(4,128)S(1)}, u32[]{:S(2)}, u32[]{:S(2)}) %collective-permute-start.10) | collective-permute-done | bytes 262176 | tf_op jit(solution)/shard_map/ppermute | solution.py:14
  59.6 12.7 %collective-permute-done.11 = f32[2,2,16,4,256]{4,3,2,1,0:T(4,128)S(1)} collective-permute-done((f32[2,2,16,4,256]{4,3,2,1,0:T(4,128)S(1)}, f32[2,2,16,4,256]{4,3,2,1,0:T(4,128)S(1)}, u32[]{:S(2)}, u32[]{:S(2)}) %collective-permute-start.11) | collective-permute-done | bytes 262176 | tf_op jit(solution)/shard_map/ppermute | solution.py:14
  72.3 4.9 %collective-permute-done.12 = f32[2,2,16,4,256]{4,3,2,1,0:T(4,128)} collective-permute-done((f32[2,2,16,4,256]{4,3,2,1,0:T(4,128)S(1)}, f32[2,2,16,4,256]{4,3,2,1,0:T(4,128)}, u32[]{:S(2)}, u32[]{:S(2)}) %collective-permute-start.12) | collective-permute-done | bytes 262176 | tf_op jit(solution)/shard_map/ppermute | solution.py:14
  77.2 21.8 %collective-permute-done.13 = f32[2,2,16,4,256]{4,3,2,1,0:T(4,128)} collective-permute-done((f32[2,2,16,4,256]{4,3,2,1,0:T(4,128)S(1)}, f32[2,2,16,4,256]{4,3,2,1,0:T(4,128)}, u32[]{:S(2)}, u32[]{:S(2)}) %collective-permute-start.13) | collective-permute-done | bytes 262176 | tf_op jit(solution)/shard_map/ppermute | solution.py:14
  99.1 9.5 %concatenate.16 = f32[2,2,16,60,256]{4,3,2,1,0:T(8,128)} concatenate(f32[2,2,16,4,256]{4,3,2,1,0:T(4,128)S(1)} %collective-permute-done, f32[2,2,16,4,256]{4,3,2,1,0:T(4,128)S(1)} %collective-permute-done.1, f32[2,2,16,4,256]{4,3,2,1,0:T(4,128)S(1)} %collective-permute-done.2, f32[2,2,16,4,256]{4,3,2,1,0:T(4,128)S(1)} %collective-permute-done.3, ...), dimensions={3} | concatenate | bytes 7864320 | tf_op jit(solution)/shard_map/concatenate | solution.py:63
  112.4 7.5 %collective-permute-start.14 = (f32[2,2,16,48,256]{4,3,2,1,0:T(8,128)S(1)}, f32[2,2,16,48,256]{4,3,2,1,0:T(8,128)}, u32[]{:S(2)}, u32[]{:S(2)}) collective-permute-start(f32[2,2,16,48,256]{4,3,2,1,0:T(8,128)S(1)} %constant_dynamic-slice_fusion), channel_id=1, source_target_pairs={{0,16},{1,17},{2,18},{3,19},{4,20},{5,21},{6,22},{7,23},{8,24},{9,... | collective-permute-start | bytes 9437192 | tf_op jit(solution)/shard_map/ppermute | solution.py:24
  121.4 44.0 %collective-permute-done.15 = f32[2,2,16,48,256]{4,3,2,1,0:T(8,128)} collective-permute-done((f32[2,2,16,48,256]{4,3,2,1,0:T(8,128)S(1)}, f32[2,2,16,48,256]{4,3,2,1,0:T(8,128)}, u32[]{:S(2)}, u32[]{:S(2)}) %collective-permute-start.15) | collective-permute-done | bytes 3145760 | tf_op jit(solution)/shard_map/ppermute | solution.py:25
  168.7 7.4 %pad_maximum_fusion = f32[2,2,48,48,256]{4,3,2,1,0:T(8,128)} fusion(f32[2,2,16,48,256]{4,3,2,1,0:T(8,128)} %collective-permute-done.15, f32[2,2,16,48,256]{4,3,2,1,0:T(8,128)S(1)} %constant_dynamic-slice_fusion, f32[2,2,16,48,256]{4,3,2,1,0:T(8,128)} %collective-permute-done.14), kind=kLoop, calls=%fused_computation.4 | loop fusion | flops 4718592 | bytes 18874368 | tf_op jit(solution)/shard_map/concatenate | solution.py:26
  176.1 4.7 %fusion.59 = (f32[1,2,48,48,256]{4,3,2,1,0:T(8,128)S(1)}, f32[1,2,48,48,256]{4,3,2,1,0:T(8,128)S(1)}) fusion(f32[2,2,48,48,256]{4,3,2,1,0:T(8,128)} %pad_maximum_fusion), kind=kLoop, calls=%fused_computation.83 | loop fusion | bytes 18874368 | tf_op jit(solution)/shard_map/slice | solution.py:109
  209.3 6.1 %copy.18 = f32[4608,256]{1,0:T(8,128)} copy(f32[4608,256]{0,1:T(8,128)} %pad_maximum_fusion.1) | data formatting | bytes 9437184 | tf_op jit(solution)/shard_map/concatenate | solution.py:57
  215.4 4.9 %pad_maximum_fusion.2 = f32[4608,256]{0,1:T(8,128)} fusion(f32[4608,128]{0,1:T(8,128)} %fusion.16, f32[4608,128]{0,1:T(8,128)} %fusion.18), kind=kLoop, calls=%fused_computation.10 | loop fusion | flops 1179648 | bytes 9437184 | tf_op jit(solution)/shard_map/concatenate | solution.py:58
  220.3 6.1 %copy.19 = f32[4608,256]{1,0:T(8,128)} copy(f32[4608,256]{0,1:T(8,128)} %pad_maximum_fusion.2) | data formatting | bytes 9437184 | tf_op jit(solution)/shard_map/concatenate | solution.py:58
  235.7 50.2 %collective-permute-done.17 = f32[2,2,16,48,256]{4,3,2,1,0:T(8,128)S(1)} collective-permute-done((f32[2,2,16,48,256]{4,3,2,1,0:T(8,128)S(1)}, f32[2,2,16,48,256]{4,3,2,1,0:T(8,128)S(1)}, u32[]{:S(2)}, u32[]{:S(2)}) %collective-permute-start.17) | collective-permute-done | bytes 3145760 | tf_op jit(solution)/shard_map/ppermute | solution.py:14
  295.5 16.1 %dynamic_update_slice.3 = f32[2,2,16,60,256]{4,3,2,1,0:T(8,128)} dynamic-update-slice(f32[2,2,16,60,256]{4,3,2,1,0:T(8,128)} %broadcast_in_dim.15, f32[2,2,16,48,256]{4,3,2,1,0:T(8,128)} %fusion.3, s32[]{:T(128)} %constant.45.clone.1, s32[]{:T(128)} %constant.45.clone.1, s32[]{:T(128)} %constant.45.clone.1, s32[]{:T(128)S(6)} %select_n.28, s32[]{:T(128)} %constant.45.clone.1) | dynamic-update-slice | bytes 6291460 | tf_op jit(solution)/shard_map/dynamic_update_slice | solution.py:124
  311.5 4.8 %fusion.60 = (f32[2,2,16,4,256]{4,3,2,1,0:T(4,128)S(1)}, f32[2,2,16,4,256]{4,3,2,1,0:T(4,128)S(1)}, f32[2,2,16,4,256]{4,3,2,1,0:T(4,128)S(1)}, f32[2,2,16,4,256]...) fusion(f32[2,2,16,60,256]{4,3,2,1,0:T(8,128)} %dynamic_update_s, ...), kind=kLoop, calls=%fused_computation.84 | loop fusion | bytes 7340032 | tf_op jit(solution)/shard_map/slice | solution.py:74
  316.3 33.1 %collective-permute-start.31 = (f32[2,2,16,4,256]{4,3,2,1,0:T(4,128)S(1)}, f32[2,2,16,4,256]{4,3,2,1,0:T(4,128)S(1)}, u32[]{:S(2)}, u32[]{:S(2)}) collective-permute-start(f32[2,2,16,4,256]{4,3,2,1,0:T(4,128)S(1)} %get-tuple-element.11), channel_id=1, source_target_pairs={{0,7},{1,8},{2,9},{3,10},{4,11},{5,12},{6,13},{7,14},{8,15},{16,23... | collective-permute-start | bytes 786440 | tf_op jit(solution)/shard_map/ppermute | solution.py:14
  366.6 6.0 %fusion.27 = f32[128,128]{0,1:T(8,128)S(1)} fusion(f32[4608,256]{1,0:T(8,128)} %bitcast.16, f32[128,4608]{1,0:T(8,128)S(1)} %copy-done.6, f32[128,4608]{1,0:T(8,128)S(1)} %copy-done.1, f32[128]{0:T(128)S(1)} %get-tuple-element.30, f32[128]{0:T(128)S(1)} %broadcast_divide_fusion, f32[128]{0:T(128)S(1)} %get-tuple-element.28), kind=kOutput, calls=%fused_computation.41 | convolution fusion | flops 908345344 | bytes 7144960 | tf_op jit(solution)/shard_map/dot_general | solution.py:52
  382.5 6.0 %fusion.24 = f32[128,128]{0,1:T(8,128)S(1)} fusion(f32[4608,256]{1,0:T(8,128)} %bitcast.17, f32[128,4608]{1,0:T(8,128)S(1)} %copy-done.4, f32[128,4608]{1,0:T(8,128)S(1)} %get-tuple-element.33, f32[128]{0:T(128)S(1)} %get-tuple-element.34, f32[128]{0:T(128)S(1)} %broadcast_divide_fusion.1, f32[128]{0:T(128)S(1)} %get-tuple-element.32), kind=kOutput, calls=%fused_computation.40 | convolution fusion | flops 908345344 | bytes 7144960 | tf_op jit(solution)/shard_map/dot_general | solution.py:52
  389.4 4.7 %collective-permute-done.21 = f32[2,2,16,4,256]{4,3,2,1,0:T(4,128)} collective-permute-done((f32[2,2,16,4,256]{4,3,2,1,0:T(4,128)}, f32[2,2,16,4,256]{4,3,2,1,0:T(4,128)}, u32[]{:S(2)}, u32[]{:S(2)}) %collective-permute-start.21) | collective-permute-done | bytes 262176 | tf_op jit(solution)/shard_map/ppermute | solution.py:14
  398.6 5.0 %collective-permute-done.19 = f32[2,2,16,4,256]{4,3,2,1,0:T(4,128)} collective-permute-done((f32[2,2,16,4,256]{4,3,2,1,0:T(4,128)S(1)}, f32[2,2,16,4,256]{4,3,2,1,0:T(4,128)}, u32[]{:S(2)}, u32[]{:S(2)}) %collective-permute-start.19) | collective-permute-done | bytes 262176 | tf_op jit(solution)/shard_map/ppermute | solution.py:14
  403.6 23.5 %collective-permute-done.18 = f32[2,2,16,4,256]{4,3,2,1,0:T(4,128)} collective-permute-done((f32[2,2,16,4,256]{4,3,2,1,0:T(4,128)S(1)}, f32[2,2,16,4,256]{4,3,2,1,0:T(4,128)}, u32[]{:S(2)}, u32[]{:S(2)}) %collective-permute-start.18) | collective-permute-done | bytes 262176 | tf_op jit(solution)/shard_map/ppermute | solution.py:14
  (122 shorter events, 124.3 us)
Async XLA Ops:
  13.0 17.2 %collective-permute-start.3 = (f32[2,2,16,4,256]{4,3,2,1,0:T(4,128)S(1)}, f32[2,2,16,4,256]{4,3,2,1,0:T(4,128)S(1)}, u32[]{:S(2)}, u32[]{:S(2)}) collective-permute-start(f32[2,2,16,4,256]{4,3,2,1,0:T(4,128)S(1)} %pad_maximum_fusion.4), channel_id=1, source_target_pairs={{0,4},{1,5},{2,6},{3,7},{4,8},{5,9},{6,10},{7,11},{8,12},{9,13},{1... | collective-permute-start | bytes 786440 | tf_op jit(solution)/shard_map/ppermute | solution.py:14
  14.4 18.6 %collective-permute-start.4 = (f32[2,2,16,4,256]{4,3,2,1,0:T(4,128)S(1)}, f32[2,2,16,4,256]{4,3,2,1,0:T(4,128)S(1)}, u32[]{:S(2)}, u32[]{:S(2)}) collective-permute-start(f32[2,2,16,4,256]{4,3,2,1,0:T(4,128)S(1)} %pad_maximum_fusion.4), channel_id=1, source_target_pairs={{0,3},{1,4},{2,5},{3,6},{4,7},{5,8},{6,9},{7,10},{8,11},{9,12},{10... | collective-permute-start | bytes 786440 | tf_op jit(solution)/shard_map/ppermute | solution.py:14
  17.5 16.8 %collective-permute-start.5 = (f32[2,2,16,4,256]{4,3,2,1,0:T(4,128)S(1)}, f32[2,2,16,4,256]{4,3,2,1,0:T(4,128)S(1)}, u32[]{:S(2)}, u32[]{:S(2)}) collective-permute-start(f32[2,2,16,4,256]{4,3,2,1,0:T(4,128)S(1)} %pad_maximum_fusion.4), channel_id=1, source_target_pairs={{0,2},{1,3},{2,4},{3,5},{4,6},{5,7},{6,8},{7,9},{8,10},{9,11},{10,... | collective-permute-start | bytes 786440 | tf_op jit(solution)/shard_map/ppermute | solution.py:14
  19.4 16.1 %collective-permute-start.6 = (f32[2,2,16,4,256]{4,3,2,1,0:T(4,128)S(1)}, f32[2,2,16,4,256]{4,3,2,1,0:T(4,128)S(1)}, u32[]{:S(2)}, u32[]{:S(2)}) collective-permute-start(f32[2,2,16,4,256]{4,3,2,1,0:T(4,128)S(1)} %pad_maximum_fusion.4), channel_id=1, source_target_pairs={{0,1},{1,2},{2,3},{3,4},{4,5},{5,6},{6,7},{7,8},{8,9},{9,10},{10,1... | collective-permute-start | bytes 786440 | tf_op jit(solution)/shard_map/ppermute | solution.py:14
  33.0 21.5 %collective-permute-start.9 = (f32[2,2,16,4,256]{4,3,2,1,0:T(4,128)S(1)}, f32[2,2,16,4,256]{4,3,2,1,0:T(4,128)S(1)}, u32[]{:S(2)}, u32[]{:S(2)}) collective-permute-start(f32[2,2,16,4,256]{4,3,2,1,0:T(4,128)S(1)} %pad_maximum_fusion.4), channel_id=1, source_target_pairs={{3,0},{4,1},{5,2},{6,3},{7,4},{8,5},{9,6},{10,7},{11,8},{12,9},{13... | collective-permute-start | bytes 786440 | tf_op jit(solution)/shard_map/ppermute | solution.py:14
  34.3 25.3 %collective-permute-start.10 = (f32[2,2,16,4,256]{4,3,2,1,0:T(4,128)S(1)}, f32[2,2,16,4,256]{4,3,2,1,0:T(4,128)S(1)}, u32[]{:S(2)}, u32[]{:S(2)}) collective-permute-start(f32[2,2,16,4,256]{4,3,2,1,0:T(4,128)S(1)} %pad_maximum_fusion.4), channel_id=1, source_target_pairs={{4,0},{5,1},{6,2},{7,3},{8,4},{9,5},{10,6},{11,7},{12,8},{13,9},{1... | collective-permute-start | bytes 786440 | tf_op jit(solution)/shard_map/ppermute | solution.py:14
  35.6 36.8 %collective-permute-start.11 = (f32[2,2,16,4,256]{4,3,2,1,0:T(4,128)S(1)}, f32[2,2,16,4,256]{4,3,2,1,0:T(4,128)S(1)}, u32[]{:S(2)}, u32[]{:S(2)}) collective-permute-start(f32[2,2,16,4,256]{4,3,2,1,0:T(4,128)S(1)} %pad_maximum_fusion.4), channel_id=1, source_target_pairs={{5,0},{6,1},{7,2},{8,3},{9,4},{10,5},{11,6},{12,7},{13,8},{14,9},{... | collective-permute-start | bytes 786440 | tf_op jit(solution)/shard_map/ppermute | solution.py:14
  36.9 40.3 %collective-permute-start.12 = (f32[2,2,16,4,256]{4,3,2,1,0:T(4,128)S(1)}, f32[2,2,16,4,256]{4,3,2,1,0:T(4,128)}, u32[]{:S(2)}, u32[]{:S(2)}) collective-permute-start(f32[2,2,16,4,256]{4,3,2,1,0:T(4,128)S(1)} %pad_maximum_fusion.4), channel_id=1, source_target_pairs={{6,0},{7,1},{8,2},{9,3},{10,4},{11,5},{12,6},{13,7},{14,8},{15,9},... | collective-permute-start | bytes 786440 | tf_op jit(solution)/shard_map/ppermute | solution.py:14
  43.0 56.0 %collective-permute-start.13 = (f32[2,2,16,4,256]{4,3,2,1,0:T(4,128)S(1)}, f32[2,2,16,4,256]{4,3,2,1,0:T(4,128)}, u32[]{:S(2)}, u32[]{:S(2)}) collective-permute-start(f32[2,2,16,4,256]{4,3,2,1,0:T(4,128)S(1)} %pad_maximum_fusion.4), channel_id=1, source_target_pairs={{7,0},{8,1},{9,2},{10,3},{11,4},{12,5},{13,6},{14,7},{15,8},{23,16... | collective-permute-start | bytes 786440 | tf_op jit(solution)/shard_map/ppermute | solution.py:14
  111.1 54.2 %collective-permute-start.15 = (f32[2,2,16,48,256]{4,3,2,1,0:T(8,128)S(1)}, f32[2,2,16,48,256]{4,3,2,1,0:T(8,128)}, u32[]{:S(2)}, u32[]{:S(2)}) collective-permute-start(f32[2,2,16,48,256]{4,3,2,1,0:T(8,128)S(1)} %constant_dynamic-slice_fusion), channel_id=1, source_target_pairs={{16,0},{17,1},{18,2},{19,3},{20,4},{21,5},{22,6},{23,7},{24,8},{25... | collective-permute-start | bytes 9437192 | tf_op jit(solution)/shard_map/ppermute | solution.py:25
  112.4 56.3 %collective-permute-start.14 = (f32[2,2,16,48,256]{4,3,2,1,0:T(8,128)S(1)}, f32[2,2,16,48,256]{4,3,2,1,0:T(8,128)}, u32[]{:S(2)}, u32[]{:S(2)}) collective-permute-start(f32[2,2,16,48,256]{4,3,2,1,0:T(8,128)S(1)} %constant_dynamic-slice_fusion), channel_id=1, source_target_pairs={{0,16},{1,17},{2,18},{3,19},{4,20},{5,21},{6,22},{7,23},{8,24},{9,... | collective-permute-start | bytes 9437192 | tf_op jit(solution)/shard_map/ppermute | solution.py:24
  230.0 55.9 %collective-permute-start.17 = (f32[2,2,16,48,256]{4,3,2,1,0:T(8,128)S(1)}, f32[2,2,16,48,256]{4,3,2,1,0:T(8,128)S(1)}, u32[]{:S(2)}, u32[]{:S(2)}) collective-permute-start(f32[2,2,16,48,256]{4,3,2,1,0:T(8,128)S(1)} %get-tuple-element.7), channel_id=1, source_target_pairs={{0,16},{1,17},{2,18},{3,19},{4,20},{5,21},{6,22},{7,23},{8,24},{9,... | collective-permute-start | bytes 9437192 | tf_op jit(solution)/shard_map/ppermute | solution.py:14
  234.4 55.8 %collective-permute-start.16 = (f32[2,2,16,48,256]{4,3,2,1,0:T(8,128)S(1)}, f32[2,2,16,48,256]{4,3,2,1,0:T(8,128)S(1)}, u32[]{:S(2)}, u32[]{:S(2)}) collective-permute-start(f32[2,2,16,48,256]{4,3,2,1,0:T(8,128)S(1)} %get-tuple-element.6), channel_id=1, source_target_pairs={{16,0},{17,1},{18,2},{19,3},{20,4},{21,5},{22,6},{23,7},{24,8},{25... | collective-permute-start | bytes 9437192 | tf_op jit(solution)/shard_map/ppermute | solution.py:14
  316.3 41.3 %collective-permute-start.31 = (f32[2,2,16,4,256]{4,3,2,1,0:T(4,128)S(1)}, f32[2,2,16,4,256]{4,3,2,1,0:T(4,128)S(1)}, u32[]{:S(2)}, u32[]{:S(2)}) collective-permute-start(f32[2,2,16,4,256]{4,3,2,1,0:T(4,128)S(1)} %get-tuple-element.11), channel_id=1, source_target_pairs={{0,7},{1,8},{2,9},{3,10},{4,11},{5,12},{6,13},{7,14},{8,15},{16,23... | collective-permute-start | bytes 786440 | tf_op jit(solution)/shard_map/ppermute | solution.py:14
  353.4 19.3 %collective-permute-start.27 = (f32[2,2,16,4,256]{4,3,2,1,0:T(4,128)S(1)}, f32[2,2,16,4,256]{4,3,2,1,0:T(4,128)S(1)}, u32[]{:S(2)}, u32[]{:S(2)}) collective-permute-start(f32[2,2,16,4,256]{4,3,2,1,0:T(4,128)S(1)} %get-tuple-element.15), channel_id=1, source_target_pairs={{0,3},{1,4},{2,5},{3,6},{4,7},{5,8},{6,9},{7,10},{8,11},{9,12},{10... | collective-permute-start | bytes 786440 | tf_op jit(solution)/shard_map/ppermute | solution.py:14
  357.7 16.3 %collective-permute-start.26 = (f32[2,2,16,4,256]{4,3,2,1,0:T(4,128)S(1)}, f32[2,2,16,4,256]{4,3,2,1,0:T(4,128)S(1)}, u32[]{:S(2)}, u32[]{:S(2)}) collective-permute-start(f32[2,2,16,4,256]{4,3,2,1,0:T(4,128)S(1)} %get-tuple-element.16), channel_id=1, source_target_pairs={{0,2},{1,3},{2,4},{3,5},{4,6},{5,7},{6,8},{7,9},{8,10},{9,11},{10,... | collective-permute-start | bytes 786440 | tf_op jit(solution)/shard_map/ppermute | solution.py:14
  359.7 18.8 %collective-permute-start.25 = (f32[2,2,16,4,256]{4,3,2,1,0:T(4,128)S(1)}, f32[2,2,16,4,256]{4,3,2,1,0:T(4,128)S(1)}, u32[]{:S(2)}, u32[]{:S(2)}) collective-permute-start(f32[2,2,16,4,256]{4,3,2,1,0:T(4,128)S(1)} %get-tuple-element.17), channel_id=1, source_target_pairs={{0,1},{1,2},{2,3},{3,4},{4,5},{5,6},{6,7},{7,8},{8,9},{9,10},{10,1... | collective-permute-start | bytes 786440 | tf_op jit(solution)/shard_map/ppermute | solution.py:14
  363.0 16.7 %collective-permute-start.24 = (f32[2,2,16,4,256]{4,3,2,1,0:T(4,128)S(1)}, f32[2,2,16,4,256]{4,3,2,1,0:T(4,128)S(1)}, u32[]{:S(2)}, u32[]{:S(2)}) collective-permute-start(f32[2,2,16,4,256]{4,3,2,1,0:T(4,128)S(1)} %get-tuple-element.18), channel_id=1, source_target_pairs={{1,0},{2,1},{3,2},{4,3},{5,4},{6,5},{7,6},{8,7},{9,8},{10,9},{11,1... | collective-permute-start | bytes 786440 | tf_op jit(solution)/shard_map/ppermute | solution.py:14
  365.0 16.0 %collective-permute-start.23 = (f32[2,2,16,4,256]{4,3,2,1,0:T(4,128)S(1)}, f32[2,2,16,4,256]{4,3,2,1,0:T(4,128)S(1)}, u32[]{:S(2)}, u32[]{:S(2)}) collective-permute-start(f32[2,2,16,4,256]{4,3,2,1,0:T(4,128)S(1)} %get-tuple-element.19), channel_id=1, source_target_pairs={{2,0},{3,1},{4,2},{5,3},{6,4},{7,5},{8,6},{9,7},{10,8},{11,9},{12,... | collective-permute-start | bytes 786440 | tf_op jit(solution)/shard_map/ppermute | solution.py:14
  372.6 16.7 %collective-permute-start.22 = (f32[2,2,16,4,256]{4,3,2,1,0:T(4,128)}, f32[2,2,16,4,256]{4,3,2,1,0:T(4,128)}, u32[]{:S(2)}, u32[]{:S(2)}) collective-permute-start(f32[2,2,16,4,256]{4,3,2,1,0:T(4,128)} %get-tuple-element.20), channel_id=1, source_target_pairs={{3,0},{4,1},{5,2},{6,3},{7,4},{8,5},{9,6},{10,7},{11,8},{12,9},{13... | collective-permute-start | bytes 786440 | tf_op jit(solution)/shard_map/ppermute | solution.py:14
  374.0 20.1 %collective-permute-start.21 = (f32[2,2,16,4,256]{4,3,2,1,0:T(4,128)}, f32[2,2,16,4,256]{4,3,2,1,0:T(4,128)}, u32[]{:S(2)}, u32[]{:S(2)}) collective-permute-start(f32[2,2,16,4,256]{4,3,2,1,0:T(4,128)} %get-tuple-element.21), channel_id=1, source_target_pairs={{4,0},{5,1},{6,2},{7,3},{8,4},{9,5},{10,6},{11,7},{12,8},{13,9},{1... | collective-permute-start | bytes 786440 | tf_op jit(solution)/shard_map/ppermute | solution.py:14
  378.4 20.2 %collective-permute-start.20 = (f32[2,2,16,4,256]{4,3,2,1,0:T(4,128)}, f32[2,2,16,4,256]{4,3,2,1,0:T(4,128)}, u32[]{:S(2)}, u32[]{:S(2)}) collective-permute-start(f32[2,2,16,4,256]{4,3,2,1,0:T(4,128)} %get-tuple-element.22), channel_id=1, source_target_pairs={{5,0},{6,1},{7,2},{8,3},{9,4},{10,5},{11,6},{12,7},{13,8},{14,9},{... | collective-permute-start | bytes 786440 | tf_op jit(solution)/shard_map/ppermute | solution.py:14
  379.7 23.9 %collective-permute-start.19 = (f32[2,2,16,4,256]{4,3,2,1,0:T(4,128)S(1)}, f32[2,2,16,4,256]{4,3,2,1,0:T(4,128)}, u32[]{:S(2)}, u32[]{:S(2)}) collective-permute-start(f32[2,2,16,4,256]{4,3,2,1,0:T(4,128)S(1)} %get-tuple-element.23), channel_id=1, source_target_pairs={{6,0},{7,1},{8,2},{9,3},{10,4},{11,5},{12,6},{13,7},{14,8},{15,9},... | collective-permute-start | bytes 786440 | tf_op jit(solution)/shard_map/ppermute | solution.py:14
  381.1 46.1 %collective-permute-start.18 = (f32[2,2,16,4,256]{4,3,2,1,0:T(4,128)S(1)}, f32[2,2,16,4,256]{4,3,2,1,0:T(4,128)}, u32[]{:S(2)}, u32[]{:S(2)}) collective-permute-start(f32[2,2,16,4,256]{4,3,2,1,0:T(4,128)S(1)} %get-tuple-element.10), channel_id=1, source_target_pairs={{7,0},{8,1},{9,2},{10,3},{11,4},{12,5},{13,6},{14,7},{15,8},{23,16... | collective-permute-start | bytes 786440 | tf_op jit(solution)/shard_map/ppermute | solution.py:14
  (27 other events, 607.0 us)
where the time goes:
time: 435 us; the launch traced here: 430 us
  waiting for transfers between devices  209 us (48%)
  starting transfers between devices  102 us (23%)
  local copies, waits for them, and re-layouts  55.2 us (13%)
  matrix products  36.5 us (8%)
  other arithmetic  26.1 us (6%)
    ppermute x30, waiting for transfers between devices, passed_along(): return lax.ppermute(block, axis, route)  161 us
    ppermute x30, starting transfers between devices, passed_along(): return lax.ppermute(block, axis, route)  93.6 us
    ppermute x1, waiting for transfers between devices, extended_2(): after = lax.ppermute(first, axis, down)  44 us
    dynamic_update_slice x1, local copies, waits for them, and re-layouts, body(): lax.dynamic_update_slice(jnp.zeros(frame_shape, jnp.float32), settled_win...  16.1 us
    dot_general x2, matrix products, tile_grads(): jnp.dot(dscores, key_head, precision=highest) * score_scale  12 us
    concatenate x1, local copies, waits for them, and re-layouts, widen(): return jnp.concatenate(pieces[:reach] + [source] + pieces[reach:], axis=3)  9.47 us
  transfers between devices with their start and end apart: 32, of which 18 were waited for; matrix products, arithmetic and copies ran while one was open for 3% of the time, Pallas kernels for 0%

commit v1 on v0

v1 whole, which is shorter than its diff:
```python
import functools

import jax
import jax.numpy as jnp
from jax import lax
from jax.experimental import pallas as pl
from jax.experimental.pallas import tpu as pltpu
from jax.sharding import PartitionSpec as P

HEADS = 2
HEAD_DIM = 128
TILE = 16
AXES = ("ha", "wa")
SCORE_SCALE = HEAD_DIM ** (-0.5)
F32 = jnp.float32
BF16 = jnp.bfloat16


def split2(x):
    high = x.astype(BF16)
    return high, (x - high.astype(F32)).astype(BF16)


def split3(x):
    high = x.astype(BF16)
    rest = x - high.astype(F32)
    mid = rest.astype(BF16)
    return high, mid, (rest - mid.astype(F32)).astype(BF16)


def nt_dot(a, b):
    return lax.dot_general(a, b, (((1,), (1,)), ((), ())), preferred_element_type=F32)


def nn_dot(a, b):
    return lax.dot_general(a, b, (((1,), (0,)), ((), ())), preferred_element_type=F32)


def flat_rows(ref, part):
    block = ref[:, part]
    return block.reshape(-1, block.shape[-1])


def score_kernel(nq, nk, *refs):
    bias = refs[0]
    qd = refs[1 : 1 + nq]
    kv = refs[1 + nq : 1 + nq + nk]
    weights, dprobs, stats = refs[1 + nq + nk : 4 + nq + nk]
    key_cat, value_cat = refs[4 + nq + nk :]
    rows = weights.shape[1] // nk
    for b in range(nk):
        k1, k2, k3 = split3(flat_rows(kv[b], 0))
        key_cat[b * rows : (b + 1) * rows] = jnp.concatenate([k1, k1, k2, k2, k1, k3], axis=1)
        v1, v2 = split2(flat_rows(kv[b], 1))
        value_cat[b * rows : (b + 1) * rows] = jnp.concatenate([v1, v1, v2, v2], axis=1)
    for i in range(nq):
        q1, q2, q3 = split3(flat_rows(qd[i], 0))
        query_cat = jnp.concatenate([q1, q2, q1, q2, q3, q1], axis=1)
        d1, d2 = split2(flat_rows(qd[i], 1))
        grad_cat = jnp.concatenate([d1, d2, d1, d2], axis=1)
        peak = None
        for b in range(nk):
            part = slice(b * rows, (b + 1) * rows)
            scores = nt_dot(key_cat[part], query_cat) + bias[b]
            weights[i, part] = scores
            top = jnp.max(scores, axis=0, keepdims=True)
            peak = top if peak is None else jnp.maximum(peak, top)
        total = jnp.zeros_like(peak)
        center = jnp.zeros_like(peak)
        for b in range(nk):
            part = slice(b * rows, (b + 1) * rows)
            w = jnp.exp(weights[i, part] - peak)
            dp = nt_dot(value_cat[part], grad_cat)
            weights[i, part] = w
            dprobs[i, part] = dp
            total += jnp.sum(w, axis=0, keepdims=True)
            center += jnp.sum(w * dp, axis=0, keepdims=True)
        stats[i] = jnp.concatenate([peak, total, center, jnp.zeros((5, peak.shape[1]), F32)], axis=0)


def grad_kernel(nq, nk, *refs):
    weights, dprobs, coef = refs[:3]
    qd = refs[3 : 3 + nq]
    kv = refs[3 + nq : 3 + nq + nk]
    outs = refs[3 + nq + nk :]
    query_out = outs[:nq]
    kv_out = outs[nq : nq + nk]
    key_acc, value_acc, key_t = outs[nq + nk :]
    rows = weights.shape[1] // nk
    for b in range(nk):
        k1, k2 = split2(flat_rows(kv[b], 0).T)
        both = jnp.concatenate([k1, k2], axis=0)
        key_t[b] = jnp.concatenate([both, both], axis=1)
    for i in range(nq):
        q1, q2 = split2(flat_rows(qd[i], 0))
        query_pair = jnp.concatenate([q1, q2], axis=1)
        query_pair = jnp.concatenate([query_pair, query_pair], axis=0)
        d1, d2 = split2(flat_rows(qd[i], 1))
        grad_pair = jnp.concatenate([d1, d2], axis=1)
        grad_pair = jnp.concatenate([grad_pair, grad_pair], axis=0)
        scale = coef[i, 0:1]
        center = coef[i, 1:2]
        query_sum = None
        for b in range(nk):
            part = slice(b * rows, (b + 1) * rows)
            p = weights[i, part] * scale
            ds = p * (dprobs[i, part] - center)
            value_part = nn_dot(jnp.concatenate(split2(p), axis=1), grad_pair)
            s1, s2 = split2(ds)
            key_part = nn_dot(jnp.concatenate([s1, s2], axis=1), query_pair)
            query_part = nn_dot(key_t[b], jnp.concatenate([s1, s2], axis=0))
            query_sum = query_part if query_sum is None else query_sum + query_part
            if i == 0:
                value_acc[part] = value_part
                key_acc[part] = key_part
            else:
                value_acc[part] += value_part
                key_acc[part] += key_part
        query_t = (query_sum[:HEAD_DIM] + query_sum[HEAD_DIM:]) * SCORE_SCALE
        query_out[i][...] = query_t.T
    for b in range(nk):
        part = slice(b * rows, (b + 1) * rows)
        kv_out[b][0] = key_acc[part, :HEAD_DIM] + key_acc[part, HEAD_DIM:]
        kv_out[b][1] = value_acc[part, :HEAD_DIM] + value_acc[part, HEAD_DIM:]


def whole_vmem(count):
    return [pl.BlockSpec(memory_space=pltpu.VMEM)] * count


def partial_scores(bias, qd, kv, rows):
    nq, nk = len(qd), len(kv)
    big = jax.ShapeDtypeStruct((nq, nk * rows, rows), F32)
    return pl.pallas_call(
        functools.partial(score_kernel, nq, nk),
        out_shape=(big, big, jax.ShapeDtypeStruct((nq, 8, rows), F32)),
        in_specs=[pl.BlockSpec(memory_space=pltpu.SMEM)] + whole_vmem(nq + nk),
        out_specs=tuple(whole_vmem(3)),
        scratch_shapes=[
            pltpu.VMEM((nk * rows, 6 * HEAD_DIM), BF16),
            pltpu.VMEM((nk * rows, 4 * HEAD_DIM), BF16),
        ],
        name="scores",
    )(bias, *qd, *kv)


def partial_grads(weights, dprobs, coef, qd, kv, rows):
    nq, nk = len(qd), len(kv)
    outs = [jax.ShapeDtypeStruct((rows, HEAD_DIM), F32)] * nq
    outs += [jax.ShapeDtypeStruct((2, rows, HEAD_DIM), F32)] * nk
    result = pl.pallas_call(
        functools.partial(grad_kernel, nq, nk),
        out_shape=tuple(outs),
        in_specs=whole_vmem(3 + nq + nk),
        out_specs=tuple(whole_vmem(nq + nk)),
        scratch_shapes=[
            pltpu.VMEM((nk * rows, 2 * HEAD_DIM), F32),
            pltpu.VMEM((nk * rows, 2 * HEAD_DIM), F32),
            pltpu.VMEM((nk, 2 * HEAD_DIM, 2 * rows), BF16),
        ],
        name="grads",
    )(weights, dprobs, coef, *qd, *kv)
    return result[:nq], result[nq:]


def body(high, wide, query_field, key_field, value_field, output_grad):
    frames, rows_local, cols_local, channels = query_field.shape
    per_tile = TILE // cols_local
    pairs = per_tile // 2
    tiles = wide // per_tile
    rows_own = frames * rows_local * cols_local
    rows = 2 * rows_own
    around = high > 2

    def moved(value, dx, dy, dz):
        route = []
        for a in range(high):
            for w in range(wide):
                tile, pair, core = w // per_tile, (w % per_tile) // 2, w % 2
                to_a = a + dy if around else (a + dy) % high
                to_tile = tile + dz
                if 0 <= to_a < high and 0 <= to_tile < tiles:
                    to_w = to_tile * per_tile + ((pair + dx) % pairs) * 2 + core
                    route.append((a * wide + w, to_a * wide + to_w))
        return lax.ppermute(value, AXES, route)

    def swapped(value):
        route = [(a * wide + w, a * wide + (w ^ 1)) for a in range(high) for w in range(wide)]
        return lax.ppermute(value, AXES, route)

    row_steps = (0, -1, 1) if around else tuple(range(high))
    places = [(dx, dy) for dy in row_steps for dx in range(pairs)]
    nq = len(places)

    width_index = lax.axis_index("wa")
    head = width_index % 2
    tile = width_index // per_tile
    stacked = jnp.stack([query_field * SCORE_SCALE, output_grad, key_field, value_field])
    stacked = stacked.reshape(4, rows_own, channels)
    kept = lax.dynamic_slice_in_dim(stacked, head * HEAD_DIM, HEAD_DIM, 2)
    sent = lax.dynamic_slice_in_dim(stacked, (1 - head) * HEAD_DIM, HEAD_DIM, 2)
    received = swapped(sent)
    qd_own = jnp.stack([kept[:2], received[:2]])
    kv_own = jnp.stack([kept[2:], received[2:]])

    qd = [qd_own] + [moved(qd_own, -dx, -dy, 0) for dx, dy in places[1:]]
    sides = [0, -1, 1]
    kv = [kv_own] + [moved(kv_own, 0, 0, -dz) for dz in sides[1:]]
    at = tile + jnp.array(sides, jnp.int32)
    bias = jnp.where((at >= 0) & (at < tiles), 0.0, -1e30).astype(F32)

    weights, dprobs, stats = partial_scores(bias, qd, kv, rows)

    if around:
        parts = [stats[0]] + [moved(stats[i], dx, dy, 0) for i, (dx, dy) in enumerate(places) if i]
        parts = jnp.stack(parts)
        seen = parts[:, 1] > 0.0
        peak = jnp.max(jnp.where(seen, parts[:, 0], -jnp.inf), axis=0)
        factor = jnp.where(seen, jnp.exp(parts[:, 0] - peak), 0.0)
        total = jnp.sum(factor * parts[:, 1], axis=0)
        center = jnp.sum(factor * parts[:, 2], axis=0) / total
        final = jnp.stack([peak, total, center])
        final = jnp.stack([final] + [moved(final, -dx, -dy, 0) for dx, dy in places[1:]])
        peak, total, center = final[:, 0], final[:, 1], final[:, 2]
        inside = total > 0.0
        scale = jnp.where(inside, jnp.exp(stats[:, 0] - peak) / jnp.where(inside, total, 1.0), 0.0)
    else:
        spot = {place: i for i, place in enumerate(places)}
        parts = []
        for dx, dy in places:
            got = stats if (dx, dy) == (0, 0) else moved(stats, -dx, -dy, 0)
            order = [spot[((x - dx) % pairs, (y - dy) % high)] for x, y in places]
            parts.append(jnp.stack([got[j] for j in order]))
        parts = jnp.stack(parts)
        peak = jnp.max(parts[:, :, 0], axis=0)
        factor = jnp.exp(parts[:, :, 0] - peak)
        total = jnp.sum(factor * parts[:, :, 1], axis=0)
        center = jnp.sum(factor * parts[:, :, 2], axis=0) / total
        scale = factor[0] / total
    coef = jnp.stack([scale, center], axis=1)

    query_parts, kv_parts = partial_grads(weights, dprobs, coef, qd, kv, rows)

    kv_sum = kv_parts[0]
    for b, dz in enumerate(sides):
        if dz:
            kv_sum = kv_sum + moved(kv_parts[b], 0, 0, dz)
    query_sum = query_parts[0]
    for i, (dx, dy) in enumerate(places):
        if i:
            query_sum = query_sum + moved(query_parts[i], dx, dy, 0)

    summed = jnp.concatenate([query_sum[None], kv_sum]).reshape(3, 2, rows_own, HEAD_DIM)
    mine = summed[:, 0]
    other = swapped(summed[:, 1])
    first = head == 0
    result = jnp.concatenate([jnp.where(first, mine, other), jnp.where(first, other, mine)], axis=2)
    result = result.reshape(3, frames, rows_local, cols_local, channels)
    return result[0], result[1], result[2]


def solution(mesh):
    placed = P(None, "ha", "wa", None)
    return jax.shard_map(
        functools.partial(body, mesh.shape["ha"], mesh.shape["wa"]),
        mesh=mesh,
        in_specs=(placed,) * 4,
        out_specs=(placed,) * 3,
        check_vma=False,
    )
```

time: 435 us -> 65.4 us (0.15)
  waiting for transfers between devices: 209 us -> 14.2 us
  starting transfers between devices: 102 us -> 23.7 us
  local copies, waits for them, and re-layouts: 55.2 us -> 7.6 us
  matrix products: 36.5 us -> 0 us
  other arithmetic: 26.1 us -> 4.35 us
  Pallas kernels: 0 us -> 13.8 us
    ppermute x32 -> x15, waiting for transfers between devices: 209 us -> 14.2 us  [the longest x13 11.6 us: moved(): return lax.ppermute(value, AXES, route)]
    ppermute x32 -> x15, starting transfers between devices: 102 us -> 23.7 us  [the longest x13 19.7 us: moved(): return lax.ppermute(value, AXES, route)]
    dot_general x10 -> x0, matrix products: 36.5 us -> none  [the longest x2 12 us: tile_grads(): jnp.dot(dscores, key_head, precision=highest) * score_scale]
    concatenate x4 -> x0, local copies, waits for them, and re-layouts: 21.7 us -> none  [the longest x1 9.47 us: widen(): return jnp.concatenate(pieces[:reach] + [source] + pieces[reach:], axis=3)]
    dynamic_update_slice x1 -> x0, local copies, waits for them, and re-layouts: 16.1 us -> none  [body(): lax.dynamic_update_slice(jnp.zeros(frame_shape, jnp.float32), settled_win...]
    concatenate x4 -> x1, other arithmetic: 15.3 us -> 0.03 us  [body(): jnp.concatenate([jnp.where(first, mine, other), jnp.where(first, other, m...]
    pallas_call x0 -> x2, Pallas kernels: none -> 13.8 us  [the longest x1 6.98 us: partial_scores(): pl.pallas_call(functools.partial(score_kernel, nq, nk), out_shape=(big, b...]
    slice x3, local copies, waits for them, and re-layouts: 9.53 us -> 0.06 us  [body(): parts.append(jnp.stack([got[j] for j in order]))]
  transfers between devices with their start and end apart: 32 -> 15, of which waited for: 18 -> 8; matrix products, arithmetic and copies ran while one was open for 3% -> 3% of each run, Pallas kernels for 0% -> 0%
where the time goes in v1:
time: 65.4 us; the launch traced here: 64.6 us
  starting transfers between devices  23.7 us (36%)
  waiting for transfers between devices  14.2 us (22%)
  Pallas kernels  13.8 us (21%)
  local copies, waits for them, and re-layouts  7.6 us (12%)
  other arithmetic  4.35 us (7%)
  between operations  0.99 us (2%)
    ppermute x13, starting transfers between devices, moved(): return lax.ppermute(value, AXES, route)  19.7 us
    ppermute x13, waiting for transfers between devices, moved(): return lax.ppermute(value, AXES, route)  11.6 us
    pallas_call x1, Pallas kernels, partial_scores(): pl.pallas_call(functools.partial(score_kernel, nq, nk), out_shape=(big, b...  6.98 us
    pallas_call x1, Pallas kernels, partial_grads(): pl.pallas_call(functools.partial(grad_kernel, nq, nk), out_shape=tuple(ou...  6.82 us
    ppermute x2, starting transfers between devices, swapped(): return lax.ppermute(value, AXES, route)  4.02 us
    another operation x5, local copies, waits for them, and re-layouts, body(): jnp.stack([query_field * SCORE_SCALE, output_grad, key_field, value_field])  2.91 us
    ppermute x2, waiting for transfers between devices, swapped(): return lax.ppermute(value, AXES, route)  2.55 us
    squeeze x3, local copies, waits for them, and re-layouts, body(): return (result[0], result[1], result[2])  2.08 us
  transfers between devices with their start and end apart: 15, of which 8 were waited for; matrix products, arithmetic and copies ran while one was open for 3% of the time, Pallas kernels for 0%

profile of v1, /device:TPU:1, one launch (start us, length us, event | category | flops | bytes accessed | tf_op | source)
XLA Modules:
  0.0 64.6 jit_solution(13976861151840780611)
XLA Ops:
  0.7 0.9 %broadcast_multiply_fusion = f32[2,16,4,256]{3,2,1,0:T(4,128)S(1)} fusion(f32[2,16,4,256]{3,2,1,0:T(4,128)} %param.5), kind=kLoop, calls=%fused_computation.23 | loop fusion | flops 32768 | bytes 262144 | tf_op jit(solution)/shard_map/mul | solution.py:198
  1.7 1.0 %stack.67 = f32[1,128,256]{2,1,0:T(8,128)S(1)} reshape(f32[2,16,4,256]{3,2,1,0:T(4,128)} %param.6) | data formatting | bytes 262144 | tf_op jit(solution)/shard_map/stack | solution.py:198
  2.6 1.0 %stack.68 = f32[1,128,256]{2,1,0:T(8,128)S(1)} reshape(f32[2,16,4,256]{3,2,1,0:T(4,128)} %param.7) | data formatting | bytes 262144 | tf_op jit(solution)/shard_map/stack | solution.py:198
  3.6 1.0 %stack.66 = f32[1,128,256]{2,1,0:T(8,128)S(1)} reshape(f32[2,16,4,256]{3,2,1,0:T(4,128)} %param.8) | data formatting | bytes 262144 | tf_op jit(solution)/shard_map/stack | solution.py:198
  4.8 1.5 %collective-permute-done = f32[4,128,128]{2,1,0:T(8,128)S(1)} collective-permute-done((f32[4,128,128]{2,1,0:T(8,128)S(1)}, f32[4,128,128]{2,1,0:T(8,128)S(1)}, u32[]{:S(2)}, u32[]{:S(2)}) %collective-permute-start) | collective-permute-done | bytes 262176 | tf_op jit(solution)/shard_map/ppermute | solution.py:189
  6.3 3.4 %collective-permute-start.3 = (f32[2,2,128,128]{3,2,1,0:T(8,128)S(1)}, f32[2,2,128,128]{3,2,1,0:T(8,128)S(1)}, u32[]{:S(2)}, u32[]{:S(2)}) collective-permute-start(f32[2,2,128,128]{3,2,1,0:T(8,128)S(1)} %pad_maximum_fusion.refs_1_.refs_3_), channel_id=1, source_target_pairs={{0,18},{1,19},{2,16},{3,17},{4,22},{5,23},{6,20},{7,21},{8,26},{9,... | collective-permute-start | bytes 786440 | tf_op jit(solution)/shard_map/ppermute | solution.py:185
  10.0 1.3 %collective-permute-start.5 = (f32[2,2,128,128]{3,2,1,0:T(8,128)S(1)}, f32[2,2,128,128]{3,2,1,0:T(8,128)S(1)}, u32[]{:S(2)}, u32[]{:S(2)}) collective-permute-start(f32[2,2,128,128]{3,2,1,0:T(8,128)S(1)} %pad_maximum_fusion.1.refs_5_.refs_7_), channel_id=1, source_target_pairs={{4,0},{5,1},{6,2},{7,3},{8,4},{9,5},{10,6},{11,7},{12,8},{13,9},{1... | collective-permute-start | bytes 786440 | tf_op jit(solution)/shard_map/ppermute | solution.py:185
  11.3 4.0 %collective-permute-start.4 = (f32[2,2,128,128]{3,2,1,0:T(8,128)S(1)}, f32[2,2,128,128]{3,2,1,0:T(8,128)S(1)}, u32[]{:S(2)}, u32[]{:S(2)}) collective-permute-start(f32[2,2,128,128]{3,2,1,0:T(8,128)S(1)} %pad_maximum_fusion.1.refs_5_.refs_7_), channel_id=1, source_target_pairs={{0,4},{1,5},{2,6},{3,7},{4,8},{5,9},{6,10},{7,11},{8,12},{9,13},{1... | collective-permute-start | bytes 786440 | tf_op jit(solution)/shard_map/ppermute | solution.py:185
  16.0 6.0 %collective-permute-done.2.refs_3_.refs_5_ = f32[2,2,128,128]{3,2,1,0:T(8,128)S(1)} collective-permute-done((f32[2,2,128,128]{3,2,1,0:T(8,128)S(1)}, f32[2,2,128,128]{3,2,1,0:T(8,128)S(1)}, u32[]{:S(2)}, u32[]{:S(2)}) %collective-permute-start.2) | collective-permute-done | bytes 262176 | tf_op jit(solution)/shard_map/ppermute | solution.py:185
  23.7 7.0 %scores.1 = (f32[4,768,256]{2,1,0:T(8,128)}, f32[4,768,256]{2,1,0:T(8,128)}, f32[4,8,256]{2,1,0:T(8,128)}) custom-call(f32[3]{0:T(128)} %and_select_fusion.refs_0_, f32[2,2,128,128]{3,2,1,0:T(8,128)} %copy-done, f32[2,2,128,128]{3,2,1,0:T(8,128)} %copy-done.4, f32[2,2,128,128]{3,2,1,0:T(8,128)} %copy-done.3, f32[2,2,128,128]{3,2,1,0:T(8,128)} %copy-done.2, ...), custom_call_target="tpu_custom_call" | custom-call | tf_op jit(solution)/shard_map/scores/pallas_call | solution.py:134
  31.4 1.5 %collective-permute-start.7 = (f32[4,8,256]{2,0,1:T(4,128)S(1)}, f32[4,8,256]{2,0,1:T(4,128)S(1)}, u32[]{:S(2)}, u32[]{:S(2)}) collective-permute-start(f32[4,8,256]{2,0,1:T(4,128)S(1)} %copy.8), channel_id=1, source_target_pairs={{0,16},{1,17},{2,18},{3,19},{4,20},{5,21},{6,22},{7,23},{8,24},{9,... | collective-permute-start | bytes 98312 | tf_op jit(solution)/shard_map/ppermute | solution.py:185
  32.9 1.2 %collective-permute-start.8 = (f32[4,8,256]{2,0,1:T(4,128)S(1)}, f32[4,8,256]{2,0,1:T(4,128)S(1)}, u32[]{:S(2)}, u32[]{:S(2)}) collective-permute-start(f32[4,8,256]{2,0,1:T(4,128)S(1)} %copy.8), channel_id=1, source_target_pairs={{0,18},{1,19},{2,16},{3,17},{4,22},{5,23},{6,20},{7,21},{8,26},{9,... | collective-permute-start | bytes 98312 | tf_op jit(solution)/shard_map/ppermute | solution.py:185
  34.3 2.4 %collective-permute-done.8 = f32[4,8,256]{2,0,1:T(4,128)S(1)} collective-permute-done((f32[4,8,256]{2,0,1:T(4,128)S(1)}, f32[4,8,256]{2,0,1:T(4,128)S(1)}, u32[]{:S(2)}, u32[]{:S(2)}) %collective-permute-start.8) | collective-permute-done | bytes 32800 | tf_op jit(solution)/shard_map/ppermute | solution.py:185
  38.1 6.8 %grads.1 = (f32[256,128]{1,0:T(8,128)}, f32[256,128]{1,0:T(8,128)}, f32[256,128]{1,0:T(8,128)}, f32[256,128]{1,0:T(8,128)}, f32[2,256,128]{2,1,0:T(8,128)}, /*in...) custom-call(f32[4,768,256]{2,1,0:T(8,128)} %get-tuple-element.13.refs_0_, f32[4,768,256]{2,1,0:T(8,128)} %get-tuple-element.14.refs_1_, ...), custom_call_target="tpu_custom_call" | custom-call | tf_op jit(solution)/shard_map/grads/pallas_call | solution.py:151
  44.9 1.3 %collective-permute-start.10 = (f32[256,128]{1,0:T(8,128)}, f32[256,128]{1,0:T(8,128)S(1)}, u32[]{:S(2)}, u32[]{:S(2)}) collective-permute-start(f32[256,128]{1,0:T(8,128)} %get-tuple-element.18), channel_id=1, source_target_pairs={{0,16},{1,17},{2,18},{3,19},{4,20},{5,21},{6,22},{7,23},{8,24},{9,... | collective-permute-start | bytes 393224 | tf_op jit(solution)/shard_map/ppermute | solution.py:185
  46.3 1.3 %collective-permute-start.11 = (f32[256,128]{1,0:T(8,128)}, f32[256,128]{1,0:T(8,128)S(1)}, u32[]{:S(2)}, u32[]{:S(2)}) collective-permute-start(f32[256,128]{1,0:T(8,128)} %get-tuple-element.19), channel_id=1, source_target_pairs={{0,18},{1,19},{2,16},{3,17},{4,22},{5,23},{6,20},{7,21},{8,26},{9,... | collective-permute-start | bytes 393224 | tf_op jit(solution)/shard_map/ppermute | solution.py:185
  47.5 1.3 %collective-permute-start.12 = (f32[2,256,128]{2,1,0:T(8,128)}, f32[2,256,128]{2,1,0:T(8,128)S(1)}, u32[]{:S(2)}, u32[]{:S(2)}) collective-permute-start(f32[2,256,128]{2,1,0:T(8,128)} %get-tuple-element.21), channel_id=1, source_target_pairs={{4,0},{5,1},{6,2},{7,3},{8,4},{9,5},{10,6},{11,7},{12,8},{13,9},{1... | collective-permute-start | bytes 786440 | tf_op jit(solution)/shard_map/ppermute | solution.py:185
  48.8 4.0 %collective-permute-start.13 = (f32[2,256,128]{2,1,0:T(8,128)}, f32[2,256,128]{2,1,0:T(8,128)S(1)}, u32[]{:S(2)}, u32[]{:S(2)}) collective-permute-start(f32[2,256,128]{2,1,0:T(8,128)} %get-tuple-element.22), channel_id=1, source_target_pairs={{0,4},{1,5},{2,6},{3,7},{4,8},{5,9},{6,10},{7,11},{8,12},{9,13},{1... | collective-permute-start | bytes 786440 | tf_op jit(solution)/shard_map/ppermute | solution.py:185
  52.9 0.9 %add_add_fusion.1 = f32[256,128]{1,0:T(8,128)S(1)} fusion(f32[256,128]{1,0:T(8,128)S(1)} %collective-permute-done.11, f32[256,128]{1,0:T(8,128)S(1)} %collective-permute-done.10, f32[256,128]{1,0:T(8,128)} %get-tuple-element.16, f32[256,128]{1,0:T(8,128)S(1)} %collective-permute-done.9), kind=kLoop, calls=%fused_computation.20 | loop fusion | flops 98304 | bytes 655360 | tf_op jit(solution)/shard_map/add | solution.py:251
  53.8 1.0 %collective-permute-done.12 = f32[2,256,128]{2,1,0:T(8,128)S(1)} collective-permute-done((f32[2,256,128]{2,1,0:T(8,128)}, f32[2,256,128]{2,1,0:T(8,128)S(1)}, u32[]{:S(2)}, u32[]{:S(2)}) %collective-permute-start.12) | collective-permute-done | bytes 262176 | tf_op jit(solution)/shard_map/ppermute | solution.py:185
  54.9 1.6 %collective-permute-done.13 = f32[2,256,128]{2,1,0:T(8,128)S(1)} collective-permute-done((f32[2,256,128]{2,1,0:T(8,128)}, f32[2,256,128]{2,1,0:T(8,128)S(1)}, u32[]{:S(2)}, u32[]{:S(2)}) %collective-permute-start.13) | collective-permute-done | bytes 262176 | tf_op jit(solution)/shard_map/ppermute | solution.py:185
  56.4 1.0 %add_add_fusion = f32[2,256,128]{2,1,0:T(8,128)S(1)} fusion(f32[2,256,128]{2,1,0:T(8,128)S(1)} %collective-permute-done.13, f32[2,256,128]{2,1,0:T(8,128)} %get-tuple-element.20, f32[2,256,128]{2,1,0:T(8,128)S(1)} %collective-permute-done.12), kind=kLoop, calls=%fused_computation.8 | loop fusion | flops 131072 | bytes 1048576 | tf_op jit(solution)/shard_map/add | solution.py:247
  57.5 3.9 %collective-permute-start.14 = (f32[3,128,128]{2,1,0:T(8,128)S(1)}, f32[3,128,128]{2,1,0:T(8,128)S(1)}, u32[]{:S(2)}, u32[]{:S(2)}) collective-permute-start(f32[3,128,128]{2,1,0:T(8,128)S(1)} %fusion.2), channel_id=1, source_target_pairs={{0,1},{1,0},{2,3},{3,2},{4,5},{5,4},{6,7},{7,6},{8,9},{9,8},{10,11... | collective-permute-start | bytes 589832 | tf_op jit(solution)/shard_map/ppermute | solution.py:189
  61.4 1.1 %collective-permute-done.14 = f32[3,128,128]{2,1,0:T(8,128)S(1)} collective-permute-done((f32[3,128,128]{2,1,0:T(8,128)S(1)}, f32[3,128,128]{2,1,0:T(8,128)S(1)}, u32[]{:S(2)}, u32[]{:S(2)}) %collective-permute-start.14) | collective-permute-done | bytes 196640 | tf_op jit(solution)/shard_map/ppermute | solution.py:189
  (62 shorter events, 7.3 us)
Async XLA Ops:
  0.6 14.7 %copy-start.7 = (s32[3]{0:T(128)S(1)}, s32[3]{0:T(128)}, u32[]{:S(2)}) copy-start(s32[3]{0:T(128)} %constant.49.clone) | copy-start | bytes 40
  4.6 1.6 %collective-permute-start = (f32[4,128,128]{2,1,0:T(8,128)S(1)}, f32[4,128,128]{2,1,0:T(8,128)S(1)}, u32[]{:S(2)}, u32[]{:S(2)}) collective-permute-start(f32[4,128,128]{2,1,0:T(8,128)S(1)} %constant_dynamic-slice_fusion), channel_id=1, source_target_pairs={{0,1},{1,0},{2,3},{3,2},{4,5},{5,4},{6,7},{7,6},{8,9},{9,8},{10,11... | collective-permute-start | bytes 786440 | tf_op jit(solution)/shard_map/ppermute | solution.py:189
  6.3 15.8 %copy-start = (f32[2,2,128,128]{3,2,1,0:T(8,128)}, f32[2,2,128,128]{3,2,1,0:T(8,128)S(1)}, u32[]{:S(2)}) copy-start(f32[2,2,128,128]{3,2,1,0:T(8,128)S(1)} %pad_maximum_fusion.refs_1_.refs_3_) | copy-start | bytes 786436
  6.3 9.7 %collective-permute-start.3 = (f32[2,2,128,128]{3,2,1,0:T(8,128)S(1)}, f32[2,2,128,128]{3,2,1,0:T(8,128)S(1)}, u32[]{:S(2)}, u32[]{:S(2)}) collective-permute-start(f32[2,2,128,128]{3,2,1,0:T(8,128)S(1)} %pad_maximum_fusion.refs_1_.refs_3_), channel_id=1, source_target_pairs={{0,18},{1,19},{2,16},{3,17},{4,22},{5,23},{6,20},{7,21},{8,26},{9,... | collective-permute-start | bytes 786440 | tf_op jit(solution)/shard_map/ppermute | solution.py:185
  9.7 12.4 %collective-permute-start.2 = (f32[2,2,128,128]{3,2,1,0:T(8,128)S(1)}, f32[2,2,128,128]{3,2,1,0:T(8,128)S(1)}, u32[]{:S(2)}, u32[]{:S(2)}) collective-permute-start(f32[2,2,128,128]{3,2,1,0:T(8,128)S(1)} %pad_maximum_fusion.refs_1_.refs_3_), channel_id=1, source_target_pairs={{0,16},{1,17},{2,18},{3,19},{4,20},{5,21},{6,22},{7,23},{8,24},{9,... | collective-permute-start | bytes 786440 | tf_op jit(solution)/shard_map/ppermute | solution.py:185
  9.9 12.2 %collective-permute-start.1 = (f32[2,2,128,128]{3,2,1,0:T(8,128)S(1)}, f32[2,2,128,128]{3,2,1,0:T(8,128)S(1)}, u32[]{:S(2)}, u32[]{:S(2)}) collective-permute-start(f32[2,2,128,128]{3,2,1,0:T(8,128)S(1)} %pad_maximum_fusion.refs_1_.refs_3_), channel_id=1, source_target_pairs={{0,2},{1,3},{2,0},{3,1},{4,6},{5,7},{6,4},{7,5},{8,10},{9,11},{10,... | collective-permute-start | bytes 786440 | tf_op jit(solution)/shard_map/ppermute | solution.py:185
  10.0 12.0 %copy-start.1 = (f32[2,2,128,128]{3,2,1,0:T(8,128)}, f32[2,2,128,128]{3,2,1,0:T(8,128)S(1)}, u32[]{:S(2)}) copy-start(f32[2,2,128,128]{3,2,1,0:T(8,128)S(1)} %pad_maximum_fusion.1.refs_5_.refs_7_) | copy-start | bytes 786436
  10.0 12.0 %collective-permute-start.5 = (f32[2,2,128,128]{3,2,1,0:T(8,128)S(1)}, f32[2,2,128,128]{3,2,1,0:T(8,128)S(1)}, u32[]{:S(2)}, u32[]{:S(2)}) collective-permute-start(f32[2,2,128,128]{3,2,1,0:T(8,128)S(1)} %pad_maximum_fusion.1.refs_5_.refs_7_), channel_id=1, source_target_pairs={{4,0},{5,1},{6,2},{7,3},{8,4},{9,5},{10,6},{11,7},{12,8},{13,9},{1... | collective-permute-start | bytes 786440 | tf_op jit(solution)/shard_map/ppermute | solution.py:185
  11.3 10.7 %collective-permute-start.4 = (f32[2,2,128,128]{3,2,1,0:T(8,128)S(1)}, f32[2,2,128,128]{3,2,1,0:T(8,128)S(1)}, u32[]{:S(2)}, u32[]{:S(2)}) collective-permute-start(f32[2,2,128,128]{3,2,1,0:T(8,128)S(1)} %pad_maximum_fusion.1.refs_5_.refs_7_), channel_id=1, source_target_pairs={{0,4},{1,5},{2,6},{3,7},{4,8},{5,9},{6,10},{7,11},{8,12},{9,13},{1... | collective-permute-start | bytes 786440 | tf_op jit(solution)/shard_map/ppermute | solution.py:185
  16.0 6.1 %copy-start.2 = (f32[2,2,128,128]{3,2,1,0:T(8,128)}, f32[2,2,128,128]{3,2,1,0:T(8,128)S(1)}, u32[]{:S(2)}) copy-start(f32[2,2,128,128]{3,2,1,0:T(8,128)S(1)} %collective-permute-done.3.refs_4_.refs_6_) | copy-start | bytes 786436
  22.0 0.7 %copy-start.3 = (f32[2,2,128,128]{3,2,1,0:T(8,128)}, f32[2,2,128,128]{3,2,1,0:T(8,128)S(1)}, u32[]{:S(2)}) copy-start(f32[2,2,128,128]{3,2,1,0:T(8,128)S(1)} %collective-permute-done.2.refs_3_.refs_5_) | copy-start | bytes 786436
  22.0 0.8 %copy-start.4 = (f32[2,2,128,128]{3,2,1,0:T(8,128)}, f32[2,2,128,128]{3,2,1,0:T(8,128)S(1)}, u32[]{:S(2)}) copy-start(f32[2,2,128,128]{3,2,1,0:T(8,128)S(1)} %collective-permute-done.1.refs_2_.refs_4_) | copy-start | bytes 786436
  22.1 0.9 %copy-start.5 = (f32[2,2,128,128]{3,2,1,0:T(8,128)}, f32[2,2,128,128]{3,2,1,0:T(8,128)S(1)}, u32[]{:S(2)}) copy-start(f32[2,2,128,128]{3,2,1,0:T(8,128)S(1)} %collective-permute-done.5.refs_7_.refs_9_) | copy-start | bytes 786436
  23.0 0.7 %copy-start.6 = (f32[2,2,128,128]{3,2,1,0:T(8,128)}, f32[2,2,128,128]{3,2,1,0:T(8,128)S(1)}, u32[]{:S(2)}) copy-start(f32[2,2,128,128]{3,2,1,0:T(8,128)S(1)} %collective-permute-done.4.refs_6_.refs_8_) | copy-start | bytes 786436
  31.4 2.8 %collective-permute-start.7 = (f32[4,8,256]{2,0,1:T(4,128)S(1)}, f32[4,8,256]{2,0,1:T(4,128)S(1)}, u32[]{:S(2)}, u32[]{:S(2)}) collective-permute-start(f32[4,8,256]{2,0,1:T(4,128)S(1)} %copy.8), channel_id=1, source_target_pairs={{0,16},{1,17},{2,18},{3,19},{4,20},{5,21},{6,22},{7,23},{8,24},{9,... | collective-permute-start | bytes 98312 | tf_op jit(solution)/shard_map/ppermute | solution.py:185
  32.9 3.7 %collective-permute-start.8 = (f32[4,8,256]{2,0,1:T(4,128)S(1)}, f32[4,8,256]{2,0,1:T(4,128)S(1)}, u32[]{:S(2)}, u32[]{:S(2)}) collective-permute-start(f32[4,8,256]{2,0,1:T(4,128)S(1)} %copy.8), channel_id=1, source_target_pairs={{0,18},{1,19},{2,16},{3,17},{4,22},{5,23},{6,20},{7,21},{8,26},{9,... | collective-permute-start | bytes 98312 | tf_op jit(solution)/shard_map/ppermute | solution.py:185
  34.1 3.1 %collective-permute-start.6 = (f32[4,8,256]{2,0,1:T(4,128)S(1)}, f32[4,8,256]{2,0,1:T(4,128)S(1)}, u32[]{:S(2)}, u32[]{:S(2)}) collective-permute-start(f32[4,8,256]{2,0,1:T(4,128)S(1)} %copy.8), channel_id=1, source_target_pairs={{0,2},{1,3},{2,0},{3,1},{4,6},{5,7},{6,4},{7,5},{8,10},{9,11},{10,... | collective-permute-start | bytes 98312 | tf_op jit(solution)/shard_map/ppermute | solution.py:185
  44.9 7.9 %collective-permute-start.9 = (f32[256,128]{1,0:T(8,128)}, f32[256,128]{1,0:T(8,128)S(1)}, u32[]{:S(2)}, u32[]{:S(2)}) collective-permute-start(f32[256,128]{1,0:T(8,128)} %get-tuple-element.17), channel_id=1, source_target_pairs={{0,2},{1,3},{2,0},{3,1},{4,6},{5,7},{6,4},{7,5},{8,10},{9,11},{10,... | collective-permute-start | bytes 393224 | tf_op jit(solution)/shard_map/ppermute | solution.py:185
  44.9 7.9 %collective-permute-start.10 = (f32[256,128]{1,0:T(8,128)}, f32[256,128]{1,0:T(8,128)S(1)}, u32[]{:S(2)}, u32[]{:S(2)}) collective-permute-start(f32[256,128]{1,0:T(8,128)} %get-tuple-element.18), channel_id=1, source_target_pairs={{0,16},{1,17},{2,18},{3,19},{4,20},{5,21},{6,22},{7,23},{8,24},{9,... | collective-permute-start | bytes 393224 | tf_op jit(solution)/shard_map/ppermute | solution.py:185
  46.3 6.6 %collective-permute-start.11 = (f32[256,128]{1,0:T(8,128)}, f32[256,128]{1,0:T(8,128)S(1)}, u32[]{:S(2)}, u32[]{:S(2)}) collective-permute-start(f32[256,128]{1,0:T(8,128)} %get-tuple-element.19), channel_id=1, source_target_pairs={{0,18},{1,19},{2,16},{3,17},{4,22},{5,23},{6,20},{7,21},{8,26},{9,... | collective-permute-start | bytes 393224 | tf_op jit(solution)/shard_map/ppermute | solution.py:185
  47.5 7.3 %collective-permute-start.12 = (f32[2,256,128]{2,1,0:T(8,128)}, f32[2,256,128]{2,1,0:T(8,128)S(1)}, u32[]{:S(2)}, u32[]{:S(2)}) collective-permute-start(f32[2,256,128]{2,1,0:T(8,128)} %get-tuple-element.21), channel_id=1, source_target_pairs={{4,0},{5,1},{6,2},{7,3},{8,4},{9,5},{10,6},{11,7},{12,8},{13,9},{1... | collective-permute-start | bytes 786440 | tf_op jit(solution)/shard_map/ppermute | solution.py:185
  48.8 7.6 %collective-permute-start.13 = (f32[2,256,128]{2,1,0:T(8,128)}, f32[2,256,128]{2,1,0:T(8,128)S(1)}, u32[]{:S(2)}, u32[]{:S(2)}) collective-permute-start(f32[2,256,128]{2,1,0:T(8,128)} %get-tuple-element.22), channel_id=1, source_target_pairs={{0,4},{1,5},{2,6},{3,7},{4,8},{5,9},{6,10},{7,11},{8,12},{9,13},{1... | collective-permute-start | bytes 786440 | tf_op jit(solution)/shard_map/ppermute | solution.py:185
  57.5 5.0 %collective-permute-start.14 = (f32[3,128,128]{2,1,0:T(8,128)S(1)}, f32[3,128,128]{2,1,0:T(8,128)S(1)}, u32[]{:S(2)}, u32[]{:S(2)}) collective-permute-start(f32[3,128,128]{2,1,0:T(8,128)S(1)} %fusion.2), channel_id=1, source_target_pairs={{0,1},{1,0},{2,3},{3,2},{4,5},{5,4},{6,7},{7,6},{8,9},{9,8},{10,11... | collective-permute-start | bytes 589832 | tf_op jit(solution)/shard_map/ppermute | solution.py:189

commit v2 on v1

--- a/solution.py
+++ b/solution.py
@@ -78,11 +78,33 @@
         stats[i] = jnp.concatenate([peak, total, center, jnp.zeros((5, peak.shape[1]), F32)], axis=0)
 
 
-def grad_kernel(nq, nk, *refs):
-    weights, dprobs, coef = refs[:3]
-    qd = refs[3 : 3 + nq]
-    kv = refs[3 + nq : 3 + nq + nk]
-    outs = refs[3 + nq + nk :]
+def pack_kernel(head, query, grad, key, value, sent, kept):
+    first = head[0] == 0
+    for n, ref in enumerate((query, grad, key, value)):
+        low = ref[..., :HEAD_DIM]
+        high = ref[..., HEAD_DIM:]
+        if n == 0:
+            low, high = low * SCORE_SCALE, high * SCORE_SCALE
+        kept[n] = jnp.where(first, low, high).reshape(-1, HEAD_DIM)
+        sent[n] = jnp.where(first, high, low).reshape(-1, HEAD_DIM)
+
+
+def unpack_kernel(head, mine, other, *outs):
+    first = head[0] == 0
+    for n, out in enumerate(outs):
+        shape = out.shape[:-1] + (HEAD_DIM,)
+        a, b = mine[n], other[n]
+        out[..., :HEAD_DIM] = jnp.where(first, a, b).reshape(shape)
+        out[..., HEAD_DIM:] = jnp.where(first, b, a).reshape(shape)
+
+
+def grad_kernel(nq, nk, orders, *refs):
+    weights, dprobs, stats = refs[:3]
+    parts = refs[3 : 3 + len(orders)]
+    refs = refs[3 + len(orders) :]
+    qd = refs[:nq]
+    kv = refs[nq : nq + nk]
+    outs = refs[nq + nk :]
     query_out = outs[:nq]
     kv_out = outs[nq : nq + nk]
     key_acc, value_acc, key_t = outs[nq + nk :]
@@ -98,8 +120,13 @@
         d1, d2 = split2(flat_rows(qd[i], 1))
         grad_pair = jnp.concatenate([d1, d2], axis=1)
         grad_pair = jnp.concatenate([grad_pair, grad_pair], axis=0)
-        scale = coef[i, 0:1]
-        center = coef[i, 1:2]
+        seen = [part[order[i]] for part, order in zip(parts, orders)]
+        peak = functools.reduce(jnp.maximum, [x[0:1] for x in seen])
+        factors = [jnp.exp(x[0:1] - peak) for x in seen]
+        total = sum(f * x[1:2] for f, x in zip(factors, seen))
+        total = jnp.where(total > 0.0, total, 1.0)
+        center = sum(f * x[2:3] for f, x in zip(factors, seen)) / total
+        scale = jnp.exp(stats[i, 0:1] - peak) / total
         query_sum = None
         for b in range(nk):
             part = slice(b * rows, (b + 1) * rows)
@@ -124,42 +151,48 @@
         kv_out[b][1] = value_acc[part, :HEAD_DIM] + value_acc[part, HEAD_DIM:]
 
 
-def whole_vmem(count):
-    return [pl.BlockSpec(memory_space=pltpu.VMEM)] * count
+def run_kernel(kernel, name, args, outs, scratch=(), scalars=0, limit=24, keep=True):
+    vmem = pl.BlockSpec(memory_space=pltpu.VMEM)
+    smem = pl.BlockSpec(memory_space=pltpu.SMEM)
+    if keep:
+        args = [a if n < scalars else pltpu.with_memory_space_constraint(a, pltpu.VMEM) for n, a in enumerate(args)]
+    return pl.pallas_call(
+        kernel,
+        out_shape=tuple(pltpu.VMEM(shape, F32) if vm else jax.ShapeDtypeStruct(shape, F32) for shape, vm in outs),
+        in_specs=[smem] * scalars + [vmem] * (len(args) - scalars),
+        out_specs=tuple([vmem] * len(outs)),
+        scratch_shapes=list(scratch),
+        compiler_params=pltpu.CompilerParams(vmem_limit_bytes=limit * 2**20),
+        name=name,
+    )(*args)
 
 
 def partial_scores(bias, qd, kv, rows):
     nq, nk = len(qd), len(kv)
-    big = jax.ShapeDtypeStruct((nq, nk * rows, rows), F32)
-    return pl.pallas_call(
+    big = ((nq, nk * rows, rows), True)
+    return run_kernel(
         functools.partial(score_kernel, nq, nk),
-        out_shape=(big, big, jax.ShapeDtypeStruct((nq, 8, rows), F32)),
-        in_specs=[pl.BlockSpec(memory_space=pltpu.SMEM)] + whole_vmem(nq + nk),
-        out_specs=tuple(whole_vmem(3)),
-        scratch_shapes=[
-            pltpu.VMEM((nk * rows, 6 * HEAD_DIM), BF16),
-            pltpu.VMEM((nk * rows, 4 * HEAD_DIM), BF16),
-        ],
-        name="scores",
-    )(bias, *qd, *kv)
-
-
-def partial_grads(weights, dprobs, coef, qd, kv, rows):
+        "scores",
+        [bias, *qd, *kv],
+        [big, big, ((nq, 8, rows), True)],
+        [pltpu.VMEM((nk * rows, 6 * HEAD_DIM), BF16), pltpu.VMEM((nk * rows, 4 * HEAD_DIM), BF16)],
+        scalars=1,
+    )
+
+
+def partial_grads(weights, dprobs, stats, parts, orders, qd, kv, rows):
     nq, nk = len(qd), len(kv)
-    outs = [jax.ShapeDtypeStruct((rows, HEAD_DIM), F32)] * nq
-    outs += [jax.ShapeDtypeStruct((2, rows, HEAD_DIM), F32)] * nk
-    result = pl.pallas_call(
-        functools.partial(grad_kernel, nq, nk),
-        out_shape=tuple(outs),
-        in_specs=whole_vmem(3 + nq + nk),
-        out_specs=tuple(whole_vmem(nq + nk)),
-        scratch_shapes=[
+    result = run_kernel(
+        functools.partial(grad_kernel, nq, nk, orders),
+        "grads",
+        [weights, dprobs, stats, *parts, *qd, *kv],
+        [((rows, HEAD_DIM), True)] * nq + [((2, rows, HEAD_DIM), True)] * nk,
+        [
             pltpu.VMEM((nk * rows, 2 * HEAD_DIM), F32),
             pltpu.VMEM((nk * rows, 2 * HEAD_DIM), F32),
             pltpu.VMEM((nk, 2 * HEAD_DIM, 2 * rows), BF16),
         ],
-        name="grads",
-    )(weights, dprobs, coef, *qd, *kv)
+    )
     return result[:nq], result[nq:]
 
 
@@ -195,10 +228,11 @@
     width_index = lax.axis_index("wa")
     head = width_index % 2
     tile = width_index // per_tile
-    stacked = jnp.stack([query_field * SCORE_SCALE, output_grad, key_field, value_field])
-    stacked = stacked.reshape(4, rows_own, channels)
-    kept = lax.dynamic_slice_in_dim(stacked, head * HEAD_DIM, HEAD_DIM, 2)
-    sent = lax.dynamic_slice_in_dim(stacked, (1 - head) * HEAD_DIM, HEAD_DIM, 2)
+    head_cell = head.astype(jnp.int32).reshape(1)
+    small = ((4, rows_own, HEAD_DIM), True)
+    sent, kept = run_kernel(
+        pack_kernel, "pack", [head_cell, query_field, output_grad, key_field, value_field], [small, small], scalars=1, keep=False
+    )
     received = swapped(sent)
     qd_own = jnp.stack([kept[:2], received[:2]])
     kv_own = jnp.stack([kept[2:], received[2:]])
@@ -218,28 +252,16 @@
         peak = jnp.max(jnp.where(seen, parts[:, 0], -jnp.inf), axis=0)
         factor = jnp.where(seen, jnp.exp(parts[:, 0] - peak), 0.0)
         total = jnp.sum(factor * parts[:, 1], axis=0)
-        center = jnp.sum(factor * parts[:, 2], axis=0) / total
-        final = jnp.stack([peak, total, center])
+        center = jnp.sum(factor * parts[:, 2], axis=0)
+        final = jnp.stack([peak, total, center] + [jnp.zeros_like(peak)] * 5)
         final = jnp.stack([final] + [moved(final, -dx, -dy, 0) for dx, dy in places[1:]])
-        peak, total, center = final[:, 0], final[:, 1], final[:, 2]
-        inside = total > 0.0
-        scale = jnp.where(inside, jnp.exp(stats[:, 0] - peak) / jnp.where(inside, total, 1.0), 0.0)
+        parts, orders = [final], [list(range(nq))]
     else:
         spot = {place: i for i, place in enumerate(places)}
-        parts = []
-        for dx, dy in places:
-            got = stats if (dx, dy) == (0, 0) else moved(stats, -dx, -dy, 0)
-            order = [spot[((x - dx) % pairs, (y - dy) % high)] for x, y in places]
-            parts.append(jnp.stack([got[j] for j in order]))
-        parts = jnp.stack(parts)
-        peak = jnp.max(parts[:, :, 0], axis=0)
-        factor = jnp.exp(parts[:, :, 0] - peak)
-        total = jnp.sum(factor * parts[:, :, 1], axis=0)
-        center = jnp.sum(factor * parts[:, :, 2], axis=0) / total
-        scale = factor[0] / total
-    coef = jnp.stack([scale, center], axis=1)
-
-    query_parts, kv_parts = partial_grads(weights, dprobs, coef, qd, kv, rows)
+        parts = [stats] + [moved(stats, -dx, -dy, 0) for dx, dy in places[1:]]
+        orders = [[spot[((x - dx) % pairs, (y - dy) % high)] for x, y in places] for dx, dy in places]
+
+    query_parts, kv_parts = partial_grads(weights, dprobs, stats, parts, orders, qd, kv, rows)
 
     kv_sum = kv_parts[0]
     for b, dz in enumerate(sides):
@@ -253,10 +275,8 @@
     summed = jnp.concatenate([query_sum[None], kv_sum]).reshape(3, 2, rows_own, HEAD_DIM)
     mine = summed[:, 0]
     other = swapped(summed[:, 1])
-    first = head == 0
-    result = jnp.concatenate([jnp.where(first, mine, other), jnp.where(first, other, mine)], axis=2)
-    result = result.reshape(3, frames, rows_local, cols_local, channels)
-    return result[0], result[1], result[2]
+    shape = (frames, rows_local, cols_local, channels)
+    return run_kernel(unpack_kernel, "unpack", [head_cell, mine, other], [(shape, False)] * 3, scalars=1)
 
 
 def solution(mesh):

time: 65.4 us -> 51.2 us (0.78)
  Pallas kernels: 13.8 us -> 6.73 us
  local copies, waits for them, and re-layouts: 7.6 us -> 3.64 us
  other arithmetic: 4.35 us -> 0.84 us
    pallas_call x2 -> x4, Pallas kernels: 13.8 us -> 6.73 us  [run_kernel(): pl.pallas_call(kernel, out_shape=tuple((pltpu.VMEM(shape, F32) if vm else...]
    another operation x9 -> x0, local copies, waits for them, and re-layouts: 3.01 us -> none  [the longest x5 2.91 us: body(): jnp.stack([query_field * SCORE_SCALE, output_grad, key_field, value_field])]
    squeeze x3 -> x0, local copies, waits for them, and re-layouts: 2.08 us -> none  [body(): return (result[0], result[1], result[2])]
    unnamed x19 -> x8, local copies, waits for them, and re-layouts: 1.61 us -> 3.61 us
    add x1, other arithmetic: 1.01 us -> 0.06 us  [body(): kv_sum = kv_sum + moved(kv_parts[b], 0, 0, dz)]
    mul x1 -> x0, other arithmetic: 0.94 us -> none  [body(): query_field * SCORE_SCALE]
    add x1, other arithmetic: 0.95 us -> 0.04 us  [body(): query_sum = query_sum + moved(query_parts[i], dx, dy, 0)]
    pallas_call x1 -> x0, local copies, waits for them, and re-layouts: 0.77 us -> none  [partial_scores(): pl.pallas_call(functools.partial(score_kernel, nq, nk), out_shape=(big, b...]
  transfers between devices with their start and end apart: 15 -> 15, of which waited for: 8 -> 8; matrix products, arithmetic and copies ran while one was open for 3% -> 1% of each run, Pallas kernels for 0% -> 0%
where the time goes in v2:
time: 51.2 us; the launch traced here: 50.6 us
  starting transfers between devices  23.8 us (46%)
  waiting for transfers between devices  14.8 us (29%)
  Pallas kernels  6.73 us (13%)
  local copies, waits for them, and re-layouts  3.64 us (7%)
  other arithmetic  0.84 us (2%)
  between operations  0.77 us (2%)
    ppermute x13, starting transfers between devices, moved(): return lax.ppermute(value, AXES, route)  19.7 us
    ppermute x13, waiting for transfers between devices, moved(): return lax.ppermute(value, AXES, route)  12.2 us
    pallas_call x4, Pallas kernels, run_kernel(): pl.pallas_call(kernel, out_shape=tuple((pltpu.VMEM(shape, F32) if vm else...  6.73 us
    ppermute x2, starting transfers between devices, swapped(): return lax.ppermute(value, AXES, route)  4.12 us
    unnamed x8, local copies, waits for them, and re-layouts  3.61 us
    ppermute x2, waiting for transfers between devices, swapped(): return lax.ppermute(value, AXES, route)  2.57 us
  transfers between devices with their start and end apart: 15, of which 8 were waited for; matrix products, arithmetic and copies ran while one was open for 1% of the time, Pallas kernels for 0%

profile of v2, /device:TPU:1, one launch (start us, length us, event | category | flops | bytes accessed | tf_op | source)
XLA Modules:
  0.0 50.6 jit_solution(14369688032925178656)
XLA Ops:
  0.7 0.9 %copy-done = f32[2,16,4,256]{3,2,1,0:T(4,128)S(1)} copy-done((f32[2,16,4,256]{3,2,1,0:T(4,128)S(1)}, f32[2,16,4,256]{3,2,1,0:T(4,128)}, u32[]{:S(2)}) %copy-start) | copy-done | bytes 131096
  1.6 0.9 %copy-done.1 = f32[2,16,4,256]{3,2,1,0:T(4,128)S(1)} copy-done((f32[2,16,4,256]{3,2,1,0:T(4,128)S(1)}, f32[2,16,4,256]{3,2,1,0:T(4,128)}, u32[]{:S(2)}) %copy-start.1) | copy-done | bytes 131096
  2.5 0.9 %copy-done.2 = f32[2,16,4,256]{3,2,1,0:T(4,128)S(1)} copy-done((f32[2,16,4,256]{3,2,1,0:T(4,128)S(1)}, f32[2,16,4,256]{3,2,1,0:T(4,128)}, u32[]{:S(2)}) %copy-start.2) | copy-done | bytes 131096
  3.4 0.9 %copy-done.3 = f32[2,16,4,256]{3,2,1,0:T(4,128)S(1)} copy-done((f32[2,16,4,256]{3,2,1,0:T(4,128)S(1)}, f32[2,16,4,256]{3,2,1,0:T(4,128)}, u32[]{:S(2)}) %copy-start.3) | copy-done | bytes 131096
  4.4 1.5 %collective-permute-done = f32[4,128,128]{2,1,0:T(8,128)S(1)} collective-permute-done((f32[4,128,128]{2,1,0:T(8,128)S(1)}, f32[4,128,128]{2,1,0:T(8,128)S(1)}, u32[]{:S(2)}, u32[]{:S(2)}) %collective-permute-start) | collective-permute-done | bytes 262176 | tf_op jit(solution)/shard_map/ppermute | solution.py:222
  6.0 3.4 %collective-permute-start.3 = (f32[2,2,128,128]{3,2,1,0:T(8,128)S(1)}, f32[2,2,128,128]{3,2,1,0:T(8,128)S(1)}, u32[]{:S(2)}, u32[]{:S(2)}) collective-permute-start(f32[2,2,128,128]{3,2,1,0:T(8,128)S(1)} %pad_maximum_fusion.refs_1_.refs_7_), channel_id=1, source_target_pairs={{0,18},{1,19},{2,16},{3,17},{4,22},{5,23},{6,20},{7,21},{8,26},{9,... | collective-permute-start | bytes 786440 | tf_op jit(solution)/shard_map/ppermute | solution.py:218
  9.7 1.3 %collective-permute-start.5 = (f32[2,2,128,128]{3,2,1,0:T(8,128)S(1)}, f32[2,2,128,128]{3,2,1,0:T(8,128)S(1)}, u32[]{:S(2)}, u32[]{:S(2)}) collective-permute-start(f32[2,2,128,128]{3,2,1,0:T(8,128)S(1)} %pad_maximum_fusion.1.refs_5_.refs_11_), channel_id=1, source_target_pairs={{4,0},{5,1},{6,2},{7,3},{8,4},{9,5},{10,6},{11,7},{12,8},{13,9},{1... | collective-permute-start | bytes 786440 | tf_op jit(solution)/shard_map/ppermute | solution.py:218
  11.0 4.0 %collective-permute-start.4 = (f32[2,2,128,128]{3,2,1,0:T(8,128)S(1)}, f32[2,2,128,128]{3,2,1,0:T(8,128)S(1)}, u32[]{:S(2)}, u32[]{:S(2)}) collective-permute-start(f32[2,2,128,128]{3,2,1,0:T(8,128)S(1)} %pad_maximum_fusion.1.refs_5_.refs_11_), channel_id=1, source_target_pairs={{0,4},{1,5},{2,6},{3,7},{4,8},{5,9},{6,10},{7,11},{8,12},{9,13},{1... | collective-permute-start | bytes 786440 | tf_op jit(solution)/shard_map/ppermute | solution.py:218
  15.7 6.0 %collective-permute-done.2.refs_3_.refs_9_ = f32[2,2,128,128]{3,2,1,0:T(8,128)S(1)} collective-permute-done((f32[2,2,128,128]{3,2,1,0:T(8,128)S(1)}, f32[2,2,128,128]{3,2,1,0:T(8,128)S(1)}, u32[]{:S(2)}, u32[]{:S(2)}) %collective-permute-start.2) | collective-permute-done | bytes 262176 | tf_op jit(solution)/shard_map/ppermute | solution.py:218
  21.7 3.1 %scores.1 = (f32[4,768,256]{2,1,0:T(8,128)S(1)}, f32[4,768,256]{2,1,0:T(8,128)S(1)}, f32[4,8,256]{2,1,0:T(8,128)S(1)}) custom-call(f32[3]{0:T(128)S(1)} %and_select_fusion.refs_0_, f32[2,2,128,128]{3,2,1,0:T(8,128)S(1)} %pad_maximum_fusion.refs_1_.refs_7_, f32[2,2,128,128]{3,2,1,0:T(8,128)S(1)} %collective-permute-done.1.refs_2_.refs_8_, ...), custom_call_target="tpu_custom_call" | custom-call | tf_op jit(solution)/shard_map/scores/pallas_call | solution.py:159
  24.8 0.9 %collective-permute-start.8 = (f32[4,8,256]{2,1,0:T(8,128)S(1)}, f32[4,8,256]{2,1,0:T(8,128)S(1)}, u32[]{:S(2)}, u32[]{:S(2)}) collective-permute-start(f32[4,8,256]{2,1,0:T(8,128)S(1)} %get-tuple-element.19.refs_2_.refs_3_), channel_id=1, source_target_pairs={{0,18},{1,19},{2,16},{3,17},{4,22},{5,23},{6,20},{7,21},{8,26},{9,... | collective-permute-start | bytes 98312 | tf_op jit(solution)/shard_map/ppermute | solution.py:218
  25.7 1.8 %collective-permute-start.7 = (f32[4,8,256]{2,1,0:T(8,128)S(1)}, f32[4,8,256]{2,1,0:T(8,128)S(1)}, u32[]{:S(2)}, u32[]{:S(2)}) collective-permute-start(f32[4,8,256]{2,1,0:T(8,128)S(1)} %get-tuple-element.19.refs_2_.refs_3_), channel_id=1, source_target_pairs={{0,16},{1,17},{2,18},{3,19},{4,20},{5,21},{6,22},{7,23},{8,24},{9,... | collective-permute-start | bytes 98312 | tf_op jit(solution)/shard_map/ppermute | solution.py:218
  27.5 1.0 %collective-permute-done.8.refs_6_ = f32[4,8,256]{2,1,0:T(8,128)S(1)} collective-permute-done((f32[4,8,256]{2,1,0:T(8,128)S(1)}, f32[4,8,256]{2,1,0:T(8,128)S(1)}, u32[]{:S(2)}, u32[]{:S(2)}) %collective-permute-start.8) | collective-permute-done | bytes 32800 | tf_op jit(solution)/shard_map/ppermute | solution.py:218
  28.9 1.6 %collective-permute-done.6.refs_4_ = f32[4,8,256]{2,1,0:T(8,128)S(1)} collective-permute-done((f32[4,8,256]{2,1,0:T(8,128)S(1)}, f32[4,8,256]{2,1,0:T(8,128)S(1)}, u32[]{:S(2)}, u32[]{:S(2)}) %collective-permute-start.6) | collective-permute-done | bytes 32800 | tf_op jit(solution)/shard_map/ppermute | solution.py:218
  30.5 2.8 %grads.1 = (f32[256,128]{1,0:T(8,128)S(1)}, f32[256,128]{1,0:T(8,128)S(1)}, f32[256,128]{1,0:T(8,128)S(1)}, f32[256,128]{1,0:T(8,128)S(1)}, f32[2,256,128]{2,1,0...) custom-call(f32[4,768,256]{2,1,0:T(8,128)S(1)} %get-tuple-element.17.refs_0_, ...), custom_call_target="tpu_custom_call" | custom-call | tf_op jit(solution)/shard_map/grads/pallas_call | solution.py:159
  33.4 1.5 %collective-permute-start.10 = (f32[256,128]{1,0:T(8,128)S(1)}, f32[256,128]{1,0:T(8,128)S(1)}, u32[]{:S(2)}, u32[]{:S(2)}) collective-permute-start(f32[256,128]{1,0:T(8,128)S(1)} %get-tuple-element.22), channel_id=1, source_target_pairs={{0,16},{1,17},{2,18},{3,19},{4,20},{5,21},{6,22},{7,23},{8,24},{9,... | collective-permute-start | bytes 393224 | tf_op jit(solution)/shard_map/ppermute | solution.py:218
  34.9 1.2 %collective-permute-start.11 = (f32[256,128]{1,0:T(8,128)S(1)}, f32[256,128]{1,0:T(8,128)S(1)}, u32[]{:S(2)}, u32[]{:S(2)}) collective-permute-start(f32[256,128]{1,0:T(8,128)S(1)} %get-tuple-element.23), channel_id=1, source_target_pairs={{0,18},{1,19},{2,16},{3,17},{4,22},{5,23},{6,20},{7,21},{8,26},{9,... | collective-permute-start | bytes 393224 | tf_op jit(solution)/shard_map/ppermute | solution.py:218
  36.1 1.3 %collective-permute-start.12 = (f32[2,256,128]{2,1,0:T(8,128)S(1)}, f32[2,256,128]{2,1,0:T(8,128)S(1)}, u32[]{:S(2)}, u32[]{:S(2)}) collective-permute-start(f32[2,256,128]{2,1,0:T(8,128)S(1)} %get-tuple-element.25), channel_id=1, source_target_pairs={{4,0},{5,1},{6,2},{7,3},{8,4},{9,5},{10,6},{11,7},{12,8},{13,9},{1... | collective-permute-start | bytes 786440 | tf_op jit(solution)/shard_map/ppermute | solution.py:218
  37.3 4.0 %collective-permute-start.13 = (f32[2,256,128]{2,1,0:T(8,128)S(1)}, f32[2,256,128]{2,1,0:T(8,128)S(1)}, u32[]{:S(2)}, u32[]{:S(2)}) collective-permute-start(f32[2,256,128]{2,1,0:T(8,128)S(1)} %get-tuple-element.26), channel_id=1, source_target_pairs={{0,4},{1,5},{2,6},{3,7},{4,8},{5,9},{6,10},{7,11},{8,12},{9,13},{1... | collective-permute-start | bytes 786440 | tf_op jit(solution)/shard_map/ppermute | solution.py:218
  41.4 1.7 %collective-permute-done.12 = f32[2,256,128]{2,1,0:T(8,128)S(1)} collective-permute-done((f32[2,256,128]{2,1,0:T(8,128)S(1)}, f32[2,256,128]{2,1,0:T(8,128)S(1)}, u32[]{:S(2)}, u32[]{:S(2)}) %collective-permute-start.12) | collective-permute-done | bytes 262176 | tf_op jit(solution)/shard_map/ppermute | solution.py:218
  43.2 1.5 %collective-permute-done.13 = f32[2,256,128]{2,1,0:T(8,128)S(1)} collective-permute-done((f32[2,256,128]{2,1,0:T(8,128)S(1)}, f32[2,256,128]{2,1,0:T(8,128)S(1)}, u32[]{:S(2)}, u32[]{:S(2)}) %collective-permute-start.13) | collective-permute-done | bytes 262176 | tf_op jit(solution)/shard_map/ppermute | solution.py:218
  44.7 4.0 %collective-permute-start.14 = (f32[3,128,128]{2,1,0:T(8,128)S(1)}, f32[3,128,128]{2,1,0:T(8,128)S(1)}, u32[]{:S(2)}, u32[]{:S(2)}) collective-permute-start(f32[3,128,128]{2,1,0:T(8,128)S(1)} %get-tuple-element.27), channel_id=1, source_target_pairs={{0,1},{1,0},{2,3},{3,2},{4,5},{5,4},{6,7},{7,6},{8,9},{9,8},{10,11... | collective-permute-start | bytes 589832 | tf_op jit(solution)/shard_map/ppermute | solution.py:222
  48.8 1.1 %collective-permute-done.14.other = f32[3,128,128]{2,1,0:T(8,128)S(1)} collective-permute-done((f32[3,128,128]{2,1,0:T(8,128)S(1)}, f32[3,128,128]{2,1,0:T(8,128)S(1)}, u32[]{:S(2)}, u32[]{:S(2)}) %collective-permute-start.14) | collective-permute-done | bytes 196640 | tf_op jit(solution)/shard_map/ppermute | solution.py:222
  49.8 0.8 %unpack.1 = (f32[2,16,4,256]{3,2,1,0:T(4,128)}, f32[2,16,4,256]{3,2,1,0:T(4,128)}, f32[2,16,4,256]{3,2,1,0:T(4,128)}) custom-call(s32[1]{0:T(128)} %bitcast.head, f32[3,128,128]{2,1,0:T(8,128)S(1)} %get-tuple-element.28.mine, f32[3,128,128]{2,1,0:T(8,128)S(1)} %collective-permute-done.14.other), custom_call_target="tpu_custom_call" | custom-call | tf_op jit(solution)/shard_map/unpack/pallas_call | solution.py:159
  (26 shorter events, 1.9 us)
Async XLA Ops:
  0.6 0.9 %copy-start = (f32[2,16,4,256]{3,2,1,0:T(4,128)S(1)}, f32[2,16,4,256]{3,2,1,0:T(4,128)}, u32[]{:S(2)}) copy-start(f32[2,16,4,256]{3,2,1,0:T(4,128)} %query.1) | copy-start | bytes 393220
  1.5 0.9 %copy-start.1 = (f32[2,16,4,256]{3,2,1,0:T(4,128)S(1)}, f32[2,16,4,256]{3,2,1,0:T(4,128)}, u32[]{:S(2)}) copy-start(f32[2,16,4,256]{3,2,1,0:T(4,128)} %grad.1) | copy-start | bytes 393220
  2.5 0.9 %copy-start.2 = (f32[2,16,4,256]{3,2,1,0:T(4,128)S(1)}, f32[2,16,4,256]{3,2,1,0:T(4,128)}, u32[]{:S(2)}) copy-start(f32[2,16,4,256]{3,2,1,0:T(4,128)} %key.1) | copy-start | bytes 393220
  3.4 0.9 %copy-start.3 = (f32[2,16,4,256]{3,2,1,0:T(4,128)S(1)}, f32[2,16,4,256]{3,2,1,0:T(4,128)}, u32[]{:S(2)}) copy-start(f32[2,16,4,256]{3,2,1,0:T(4,128)} %value.1) | copy-start | bytes 393220
  4.3 1.6 %collective-permute-start = (f32[4,128,128]{2,1,0:T(8,128)S(1)}, f32[4,128,128]{2,1,0:T(8,128)S(1)}, u32[]{:S(2)}, u32[]{:S(2)}) collective-permute-start(f32[4,128,128]{2,1,0:T(8,128)S(1)} %get-tuple-element.16), channel_id=1, source_target_pairs={{0,1},{1,0},{2,3},{3,2},{4,5},{5,4},{6,7},{7,6},{8,9},{9,8},{10,11... | collective-permute-start | bytes 786440 | tf_op jit(solution)/shard_map/ppermute | solution.py:222
  6.0 9.7 %collective-permute-start.3 = (f32[2,2,128,128]{3,2,1,0:T(8,128)S(1)}, f32[2,2,128,128]{3,2,1,0:T(8,128)S(1)}, u32[]{:S(2)}, u32[]{:S(2)}) collective-permute-start(f32[2,2,128,128]{3,2,1,0:T(8,128)S(1)} %pad_maximum_fusion.refs_1_.refs_7_), channel_id=1, source_target_pairs={{0,18},{1,19},{2,16},{3,17},{4,22},{5,23},{6,20},{7,21},{8,26},{9,... | collective-permute-start | bytes 786440 | tf_op jit(solution)/shard_map/ppermute | solution.py:218
  9.3 12.4 %collective-permute-start.2 = (f32[2,2,128,128]{3,2,1,0:T(8,128)S(1)}, f32[2,2,128,128]{3,2,1,0:T(8,128)S(1)}, u32[]{:S(2)}, u32[]{:S(2)}) collective-permute-start(f32[2,2,128,128]{3,2,1,0:T(8,128)S(1)} %pad_maximum_fusion.refs_1_.refs_7_), channel_id=1, source_target_pairs={{0,16},{1,17},{2,18},{3,19},{4,20},{5,21},{6,22},{7,23},{8,24},{9,... | collective-permute-start | bytes 786440 | tf_op jit(solution)/shard_map/ppermute | solution.py:218
  9.6 12.2 %collective-permute-start.1 = (f32[2,2,128,128]{3,2,1,0:T(8,128)S(1)}, f32[2,2,128,128]{3,2,1,0:T(8,128)S(1)}, u32[]{:S(2)}, u32[]{:S(2)}) collective-permute-start(f32[2,2,128,128]{3,2,1,0:T(8,128)S(1)} %pad_maximum_fusion.refs_1_.refs_7_), channel_id=1, source_target_pairs={{0,2},{1,3},{2,0},{3,1},{4,6},{5,7},{6,4},{7,5},{8,10},{9,11},{10,... | collective-permute-start | bytes 786440 | tf_op jit(solution)/shard_map/ppermute | solution.py:218
  9.7 12.0 %collective-permute-start.5 = (f32[2,2,128,128]{3,2,1,0:T(8,128)S(1)}, f32[2,2,128,128]{3,2,1,0:T(8,128)S(1)}, u32[]{:S(2)}, u32[]{:S(2)}) collective-permute-start(f32[2,2,128,128]{3,2,1,0:T(8,128)S(1)} %pad_maximum_fusion.1.refs_5_.refs_11_), channel_id=1, source_target_pairs={{4,0},{5,1},{6,2},{7,3},{8,4},{9,5},{10,6},{11,7},{12,8},{13,9},{1... | collective-permute-start | bytes 786440 | tf_op jit(solution)/shard_map/ppermute | solution.py:218
  11.0 10.7 %collective-permute-start.4 = (f32[2,2,128,128]{3,2,1,0:T(8,128)S(1)}, f32[2,2,128,128]{3,2,1,0:T(8,128)S(1)}, u32[]{:S(2)}, u32[]{:S(2)}) collective-permute-start(f32[2,2,128,128]{3,2,1,0:T(8,128)S(1)} %pad_maximum_fusion.1.refs_5_.refs_11_), channel_id=1, source_target_pairs={{0,4},{1,5},{2,6},{3,7},{4,8},{5,9},{6,10},{7,11},{8,12},{9,13},{1... | collective-permute-start | bytes 786440 | tf_op jit(solution)/shard_map/ppermute | solution.py:218
  24.8 3.7 %collective-permute-start.8 = (f32[4,8,256]{2,1,0:T(8,128)S(1)}, f32[4,8,256]{2,1,0:T(8,128)S(1)}, u32[]{:S(2)}, u32[]{:S(2)}) collective-permute-start(f32[4,8,256]{2,1,0:T(8,128)S(1)} %get-tuple-element.19.refs_2_.refs_3_), channel_id=1, source_target_pairs={{0,18},{1,19},{2,16},{3,17},{4,22},{5,23},{6,20},{7,21},{8,26},{9,... | collective-permute-start | bytes 98312 | tf_op jit(solution)/shard_map/ppermute | solution.py:218
  25.7 3.2 %collective-permute-start.7 = (f32[4,8,256]{2,1,0:T(8,128)S(1)}, f32[4,8,256]{2,1,0:T(8,128)S(1)}, u32[]{:S(2)}, u32[]{:S(2)}) collective-permute-start(f32[4,8,256]{2,1,0:T(8,128)S(1)} %get-tuple-element.19.refs_2_.refs_3_), channel_id=1, source_target_pairs={{0,16},{1,17},{2,18},{3,19},{4,20},{5,21},{6,22},{7,23},{8,24},{9,... | collective-permute-start | bytes 98312 | tf_op jit(solution)/shard_map/ppermute | solution.py:218
  27.5 3.1 %collective-permute-start.6 = (f32[4,8,256]{2,1,0:T(8,128)S(1)}, f32[4,8,256]{2,1,0:T(8,128)S(1)}, u32[]{:S(2)}, u32[]{:S(2)}) collective-permute-start(f32[4,8,256]{2,1,0:T(8,128)S(1)} %get-tuple-element.19.refs_2_.refs_3_), channel_id=1, source_target_pairs={{0,2},{1,3},{2,0},{3,1},{4,6},{5,7},{6,4},{7,5},{8,10},{9,11},{10,... | collective-permute-start | bytes 98312 | tf_op jit(solution)/shard_map/ppermute | solution.py:218
  33.3 8.0 %collective-permute-start.9 = (f32[256,128]{1,0:T(8,128)S(1)}, f32[256,128]{1,0:T(8,128)S(1)}, u32[]{:S(2)}, u32[]{:S(2)}) collective-permute-start(f32[256,128]{1,0:T(8,128)S(1)} %get-tuple-element.21), channel_id=1, source_target_pairs={{0,2},{1,3},{2,0},{3,1},{4,6},{5,7},{6,4},{7,5},{8,10},{9,11},{10,... | collective-permute-start | bytes 393224 | tf_op jit(solution)/shard_map/ppermute | solution.py:218
  33.4 7.9 %collective-permute-start.10 = (f32[256,128]{1,0:T(8,128)S(1)}, f32[256,128]{1,0:T(8,128)S(1)}, u32[]{:S(2)}, u32[]{:S(2)}) collective-permute-start(f32[256,128]{1,0:T(8,128)S(1)} %get-tuple-element.22), channel_id=1, source_target_pairs={{0,16},{1,17},{2,18},{3,19},{4,20},{5,21},{6,22},{7,23},{8,24},{9,... | collective-permute-start | bytes 393224 | tf_op jit(solution)/shard_map/ppermute | solution.py:218
  34.9 6.5 %collective-permute-start.11 = (f32[256,128]{1,0:T(8,128)S(1)}, f32[256,128]{1,0:T(8,128)S(1)}, u32[]{:S(2)}, u32[]{:S(2)}) collective-permute-start(f32[256,128]{1,0:T(8,128)S(1)} %get-tuple-element.23), channel_id=1, source_target_pairs={{0,18},{1,19},{2,16},{3,17},{4,22},{5,23},{6,20},{7,21},{8,26},{9,... | collective-permute-start | bytes 393224 | tf_op jit(solution)/shard_map/ppermute | solution.py:218
  36.1 7.1 %collective-permute-start.12 = (f32[2,256,128]{2,1,0:T(8,128)S(1)}, f32[2,256,128]{2,1,0:T(8,128)S(1)}, u32[]{:S(2)}, u32[]{:S(2)}) collective-permute-start(f32[2,256,128]{2,1,0:T(8,128)S(1)} %get-tuple-element.25), channel_id=1, source_target_pairs={{4,0},{5,1},{6,2},{7,3},{8,4},{9,5},{10,6},{11,7},{12,8},{13,9},{1... | collective-permute-start | bytes 786440 | tf_op jit(solution)/shard_map/ppermute | solution.py:218
  37.3 7.3 %collective-permute-start.13 = (f32[2,256,128]{2,1,0:T(8,128)S(1)}, f32[2,256,128]{2,1,0:T(8,128)S(1)}, u32[]{:S(2)}, u32[]{:S(2)}) collective-permute-start(f32[2,256,128]{2,1,0:T(8,128)S(1)} %get-tuple-element.26), channel_id=1, source_target_pairs={{0,4},{1,5},{2,6},{3,7},{4,8},{5,9},{6,10},{7,11},{8,12},{9,13},{1... | collective-permute-start | bytes 786440 | tf_op jit(solution)/shard_map/ppermute | solution.py:218
  44.7 5.1 %collective-permute-start.14 = (f32[3,128,128]{2,1,0:T(8,128)S(1)}, f32[3,128,128]{2,1,0:T(8,128)S(1)}, u32[]{:S(2)}, u32[]{:S(2)}) collective-permute-start(f32[3,128,128]{2,1,0:T(8,128)S(1)} %get-tuple-element.27), channel_id=1, source_target_pairs={{0,1},{1,0},{2,3},{3,2},{4,5},{5,4},{6,7},{7,6},{8,9},{9,8},{10,11... | collective-permute-start | bytes 589832 | tf_op jit(solution)/shard_map/ppermute | solution.py:222
